TPU v7x, 128 devices: a whole 4x4x4 slice. The times are simulated.
128 devices in a mesh: filt: 4 (over x), dom: 32 (over y, z, core).
Axes of the slice: x: 4, y: 4, z: 4, core: 2. Of those that a mesh axis runs over, the one named last changes fastest.
Arguments:
- log_weights: float32 [2097152], P(('filt', 'dom')), parts along dimension 0, may hold values from -20 to 250, as said below
- bins: int32 [2097152], P(('filt', 'dom')), parts along dimension 0, may hold values from 0 to 4095
- states: bfloat16 [128, 2097152], P(None, ('filt', 'dom')), parts along dimension 1, may hold values from -6 to 6
Outputs:
- cumulative: float32 [16384], P(('filt', 'dom')), parts along dimension 0
- bin_means: float32 [128, 16384], P(None, ('filt', 'dom')), parts along dimension 1
- particle_weights: float32 [2097152], P(('filt', 'dom')), parts along dimension 0
There are 4 independent parts, one for each index of `filt`. A program takes and returns all parts, laid end to end along the dimension named above; each array names one. Nothing has to cross between parts.
Inputs may be any that keep to these rules, and one draw needn't show every extreme that they name: `log_weights`: finite log-weights.
All inputs are finite; a program needn't handle non-finite values.
Results may differ from a plain program's by a relative error of at most 0.00051.
Values sent between devices are 32-bit elements; how exact they have to be, the bound alone decides.
A program may use at most 64 MiB of HBM per device.

v0:
```python
import jax
import jax.numpy as jnp
from jax import lax
from jax.sharding import PartitionSpec as P

BINS = 4096


floor_value = -10000.0


def rows_first(arrays, axis, dims):
    turned = [jnp.moveaxis(a, dim, 0) for a, dim in zip(arrays, dims)]
    both = jnp.concatenate([t.reshape(len(t), -1) for t in turned], axis=1)
    out, at, finished = (lax.all_gather(both, axis, axis=0, tiled=True), 0, [])
    for t, dim in zip(turned, dims):
        piece = out[:, at : at + t[0].size].reshape(-1, *t.shape[1:])
        finished.append(jnp.moveaxis(piece, 0, dim))
        at += t[0].size
    return tuple(finished)


def local_pairs(log_weights, bins, states):
    count = log_weights.shape[0]
    width = min(count, 1024)
    blocks = count // width
    labels = lax.iota(jnp.int32, BINS)

    def top_step(index, carry):
        start = index * width
        row_weights = lax.dynamic_slice_in_dim(log_weights, start, width)
        row_bins = lax.dynamic_slice_in_dim(bins, start, width)
        member = row_bins[:, None] == labels[None, :]
        return jnp.maximum(
            carry, jnp.max(jnp.where(member, row_weights[:, None], floor_value), axis=0)
        )

    bin_top = lax.fori_loop(0, blocks, top_step, jnp.full((BINS,), floor_value, jnp.float32))
    ones_row = jnp.ones((1, width), jnp.bfloat16)

    def sum_step(index, carry):
        totals, sums = carry
        start = index * width
        row_weights = lax.dynamic_slice_in_dim(log_weights, start, width)
        row_bins = lax.dynamic_slice_in_dim(bins, start, width)
        row_states = lax.dynamic_slice_in_dim(states, start, width, 1)
        member = row_bins[:, None] == labels[None, :]
        own_top = jnp.take(bin_top, row_bins)
        scaled = jnp.exp(row_weights - own_top).astype(jnp.bfloat16)
        spread = jnp.where(member, scaled[:, None], jnp.zeros((), jnp.bfloat16))
        totals = totals + jnp.dot(ones_row, spread, preferred_element_type=jnp.float32)[0]
        sums = sums + jnp.dot(row_states, spread, preferred_element_type=jnp.float32)
        return (totals, sums)

    start_pair = (jnp.zeros((BINS,), jnp.float32), jnp.zeros((states.shape[0], BINS), jnp.float32))
    totals, sums = lax.fori_loop(0, blocks, sum_step, start_pair)
    return (bin_top, totals, sums)


def body(log_weights, bins, states):
    groups = lax.axis_size("dom")
    owned = BINS // groups
    bin_top, totals, sums = local_pairs(log_weights, bins, states)
    top_pieces, mass_pieces, sum_pieces = (
        lax.all_to_all(bin_top[None, :], "dom", split_axis=1, concat_axis=0, tiled=True),
        lax.all_to_all(totals[None, :], "dom", split_axis=1, concat_axis=0, tiled=True),
        lax.all_to_all(sums, "dom", split_axis=1, concat_axis=0, tiled=True),
    )
    sum_pieces = sum_pieces.reshape(groups, sums.shape[0], owned)
    owned_top = jnp.max(top_pieces, axis=0)
    factor = jnp.exp(top_pieces - owned_top[None, :])
    owned_mass = jnp.sum(mass_pieces * factor, axis=0)
    owned_sums = jnp.sum(sum_pieces * factor[:, None, :], axis=0)
    block_top = jnp.max(owned_top)
    block_mass = jnp.sum(owned_mass * jnp.exp(owned_top - block_top))
    share = None
    all_tops, all_masses = rows_first((block_top[None], block_mass[None]), "dom", (0, 0))
    top = jnp.max(all_tops)
    scaled_masses = all_masses * jnp.exp(all_tops - top)
    total = jnp.sum(scaled_masses)
    lower = lax.iota(jnp.int32, groups) < lax.axis_index("dom")
    before = jnp.sum(jnp.where(lower, scaled_masses, jnp.float32(0.0)))
    share = owned_mass * jnp.exp(owned_top - top)
    cumulative = (before + jnp.cumsum(share)) / total
    bin_means = owned_sums / jnp.maximum(owned_mass, 1.0)[None, :]
    whole_count = log_weights.shape[0] * groups
    particle_weights = whole_count * jnp.exp(log_weights - top) / total
    return (cumulative, bin_means, particle_weights)


def solution(mesh):
    placed = (P(("filt", "dom")), P(("filt", "dom")), P(None, ("filt", "dom")))
    return jax.shard_map(
        body,
        mesh=mesh,
        in_specs=placed,
        out_specs=(P(("filt", "dom")), P(None, ("filt", "dom")), P(("filt", "dom"))),
        check_vma=False,
    )
```

profile of v0, /device:TPU:1, one launch (start us, length us, event | category | flops | bytes accessed | tf_op | source)
XLA Modules:
  0.0 423.3 jit_solution(10603999577651719019)
XLA Ops:
  0.7 152.2 %while.30 = (s32[]{:T(128)}, f32[4096]{0:T(1024)}, s32[16384]{0:T(1024)}, f32[16384]{0:T(1024)}, s32[]{:T(128)}, /*index=5*/s32[]{:T(128)}, s32[]{:T(128)}, s32[]{:T(128)}) while((s32[]{:T(128)}, f32[4096]{0:T(1024)}, s32[16384]{0:T(1024)}, f32[16384]{0:T(1024)}, s32[]{:T(128)}, /*index=5*/s32[]{:T(128)}, s32[]{:T(128)}, ...), condition=%wide.region_2.3_spmd.clone, body=%wide.region_0.2_spmd.clone.sunk | while | flops 12587015 | bytes 90269 | solution.py:38
  2.1 6.8 %select_reduce_fusion.2 = f32[4096]{0:T(1024)S(1)} fusion(f32[1024]{0:T(1024)S(1)} %dynamic_slice.49, s32[1024]{0:T(1024)S(1)} %dynamic_slice.50), kind=kLoop, calls=%fused_computation.4.clone.1 | loop fusion | flops 12578816 | bytes 24576 | tf_op jit(solution)/shard_map/while/body/eval_jaxpr/reduce_max | solution.py:35
  10.9 6.8 %select_reduce_fusion.2 = f32[4096]{0:T(1024)S(1)} fusion(f32[1024]{0:T(1024)S(1)} %dynamic_slice.49, s32[1024]{0:T(1024)S(1)} %dynamic_slice.50), kind=kLoop, calls=%fused_computation.4.clone.1 | loop fusion | flops 12578816 | bytes 24576 | tf_op jit(solution)/shard_map/while/body/eval_jaxpr/reduce_max | solution.py:35
  20.4 6.8 %select_reduce_fusion.2 = f32[4096]{0:T(1024)S(1)} fusion(f32[1024]{0:T(1024)S(1)} %dynamic_slice.49, s32[1024]{0:T(1024)S(1)} %dynamic_slice.50), kind=kLoop, calls=%fused_computation.4.clone.1 | loop fusion | flops 12578816 | bytes 24576 | tf_op jit(solution)/shard_map/while/body/eval_jaxpr/reduce_max | solution.py:35
  30.0 6.8 %select_reduce_fusion.2 = f32[4096]{0:T(1024)S(1)} fusion(f32[1024]{0:T(1024)S(1)} %dynamic_slice.49, s32[1024]{0:T(1024)S(1)} %dynamic_slice.50), kind=kLoop, calls=%fused_computation.4.clone.1 | loop fusion | flops 12578816 | bytes 24576 | tf_op jit(solution)/shard_map/while/body/eval_jaxpr/reduce_max | solution.py:35
  39.6 6.8 %select_reduce_fusion.2 = f32[4096]{0:T(1024)S(1)} fusion(f32[1024]{0:T(1024)S(1)} %dynamic_slice.49, s32[1024]{0:T(1024)S(1)} %dynamic_slice.50), kind=kLoop, calls=%fused_computation.4.clone.1 | loop fusion | flops 12578816 | bytes 24576 | tf_op jit(solution)/shard_map/while/body/eval_jaxpr/reduce_max | solution.py:35
  49.1 6.8 %select_reduce_fusion.2 = f32[4096]{0:T(1024)S(1)} fusion(f32[1024]{0:T(1024)S(1)} %dynamic_slice.49, s32[1024]{0:T(1024)S(1)} %dynamic_slice.50), kind=kLoop, calls=%fused_computation.4.clone.1 | loop fusion | flops 12578816 | bytes 24576 | tf_op jit(solution)/shard_map/while/body/eval_jaxpr/reduce_max | solution.py:35
  58.7 6.8 %select_reduce_fusion.2 = f32[4096]{0:T(1024)S(1)} fusion(f32[1024]{0:T(1024)S(1)} %dynamic_slice.49, s32[1024]{0:T(1024)S(1)} %dynamic_slice.50), kind=kLoop, calls=%fused_computation.4.clone.1 | loop fusion | flops 12578816 | bytes 24576 | tf_op jit(solution)/shard_map/while/body/eval_jaxpr/reduce_max | solution.py:35
  68.2 6.8 %select_reduce_fusion.2 = f32[4096]{0:T(1024)S(1)} fusion(f32[1024]{0:T(1024)S(1)} %dynamic_slice.49, s32[1024]{0:T(1024)S(1)} %dynamic_slice.50), kind=kLoop, calls=%fused_computation.4.clone.1 | loop fusion | flops 12578816 | bytes 24576 | tf_op jit(solution)/shard_map/while/body/eval_jaxpr/reduce_max | solution.py:35
  77.8 6.8 %select_reduce_fusion.2 = f32[4096]{0:T(1024)S(1)} fusion(f32[1024]{0:T(1024)S(1)} %dynamic_slice.49, s32[1024]{0:T(1024)S(1)} %dynamic_slice.50), kind=kLoop, calls=%fused_computation.4.clone.1 | loop fusion | flops 12578816 | bytes 24576 | tf_op jit(solution)/shard_map/while/body/eval_jaxpr/reduce_max | solution.py:35
  87.3 6.8 %select_reduce_fusion.2 = f32[4096]{0:T(1024)S(1)} fusion(f32[1024]{0:T(1024)S(1)} %dynamic_slice.49, s32[1024]{0:T(1024)S(1)} %dynamic_slice.50), kind=kLoop, calls=%fused_computation.4.clone.1 | loop fusion | flops 12578816 | bytes 24576 | tf_op jit(solution)/shard_map/while/body/eval_jaxpr/reduce_max | solution.py:35
  96.9 6.8 %select_reduce_fusion.2 = f32[4096]{0:T(1024)S(1)} fusion(f32[1024]{0:T(1024)S(1)} %dynamic_slice.49, s32[1024]{0:T(1024)S(1)} %dynamic_slice.50), kind=kLoop, calls=%fused_computation.4.clone.1 | loop fusion | flops 12578816 | bytes 24576 | tf_op jit(solution)/shard_map/while/body/eval_jaxpr/reduce_max | solution.py:35
  106.4 6.8 %select_reduce_fusion.2 = f32[4096]{0:T(1024)S(1)} fusion(f32[1024]{0:T(1024)S(1)} %dynamic_slice.49, s32[1024]{0:T(1024)S(1)} %dynamic_slice.50), kind=kLoop, calls=%fused_computation.4.clone.1 | loop fusion | flops 12578816 | bytes 24576 | tf_op jit(solution)/shard_map/while/body/eval_jaxpr/reduce_max | solution.py:35
  116.0 6.8 %select_reduce_fusion.2 = f32[4096]{0:T(1024)S(1)} fusion(f32[1024]{0:T(1024)S(1)} %dynamic_slice.49, s32[1024]{0:T(1024)S(1)} %dynamic_slice.50), kind=kLoop, calls=%fused_computation.4.clone.1 | loop fusion | flops 12578816 | bytes 24576 | tf_op jit(solution)/shard_map/while/body/eval_jaxpr/reduce_max | solution.py:35
  125.5 6.8 %select_reduce_fusion.2 = f32[4096]{0:T(1024)S(1)} fusion(f32[1024]{0:T(1024)S(1)} %dynamic_slice.49, s32[1024]{0:T(1024)S(1)} %dynamic_slice.50), kind=kLoop, calls=%fused_computation.4.clone.1 | loop fusion | flops 12578816 | bytes 24576 | tf_op jit(solution)/shard_map/while/body/eval_jaxpr/reduce_max | solution.py:35
  135.1 6.8 %select_reduce_fusion.2 = f32[4096]{0:T(1024)S(1)} fusion(f32[1024]{0:T(1024)S(1)} %dynamic_slice.49, s32[1024]{0:T(1024)S(1)} %dynamic_slice.50), kind=kLoop, calls=%fused_computation.4.clone.1 | loop fusion | flops 12578816 | bytes 24576 | tf_op jit(solution)/shard_map/while/body/eval_jaxpr/reduce_max | solution.py:35
  144.6 6.8 %select_reduce_fusion.2 = f32[4096]{0:T(1024)S(1)} fusion(f32[1024]{0:T(1024)S(1)} %dynamic_slice.49, s32[1024]{0:T(1024)S(1)} %dynamic_slice.50), kind=kLoop, calls=%fused_computation.4.clone.1 | loop fusion | flops 12578816 | bytes 24576 | tf_op jit(solution)/shard_map/while/body/eval_jaxpr/reduce_max | solution.py:35
  152.8 189.3 %while.31 = (s32[]{:T(128)}, f32[4096]{0:T(1024)S(1)}, f32[128,4096]{1,0:T(8,128)S(1)}, s32[16384]{0:T(1024)}, f32[16384]{0:T(1024)}, /*index=5*/f32[4096]{0:T(1...) while((s32[]{:T(128)}, f32[4096]{0:T(1024)S(1)}, ...), condition=%wide.region_5.6_spmd.clone, body=%wide.region_4.5_spmd.clone.sunk | while | flops 1099977728 | bytes 4573370 | solution.py:56
  153.5 5.7 %gather_fusion = f32[1024]{0:T(1024)S(1)} fusion(f32[4096]{0:T(1024)} %get-tuple-element.438, s32[1024]{0:T(1024)S(1)} %get-tuple-element.386), kind=kCustom, calls=%fused_computation.clone.clone.1 | custom fusion | bytes 12288 | tf_op jit(solution)/shard_map/while/body/eval_jaxpr/jit(_take)/gather | solution.py:48
  161.4 3.2 fusion.41
  165.4 5.7 %gather_fusion = f32[1024]{0:T(1024)S(1)} fusion(f32[4096]{0:T(1024)} %get-tuple-element.438, s32[1024]{0:T(1024)S(1)} %get-tuple-element.386), kind=kCustom, calls=%fused_computation.clone.clone.1 | custom fusion | bytes 12288 | tf_op jit(solution)/shard_map/while/body/eval_jaxpr/jit(_take)/gather | solution.py:48
  177.2 5.7 %gather_fusion = f32[1024]{0:T(1024)S(1)} fusion(f32[4096]{0:T(1024)} %get-tuple-element.438, s32[1024]{0:T(1024)S(1)} %get-tuple-element.386), kind=kCustom, calls=%fused_computation.clone.clone.1 | custom fusion | bytes 12288 | tf_op jit(solution)/shard_map/while/body/eval_jaxpr/jit(_take)/gather | solution.py:48
  185.1 3.2 fusion.41
  189.0 5.7 %gather_fusion = f32[1024]{0:T(1024)S(1)} fusion(f32[4096]{0:T(1024)} %get-tuple-element.438, s32[1024]{0:T(1024)S(1)} %get-tuple-element.386), kind=kCustom, calls=%fused_computation.clone.clone.1 | custom fusion | bytes 12288 | tf_op jit(solution)/shard_map/while/body/eval_jaxpr/jit(_take)/gather | solution.py:48
  196.9 3.2 fusion.41
  200.9 5.7 %gather_fusion = f32[1024]{0:T(1024)S(1)} fusion(f32[4096]{0:T(1024)} %get-tuple-element.438, s32[1024]{0:T(1024)S(1)} %get-tuple-element.386), kind=kCustom, calls=%fused_computation.clone.clone.1 | custom fusion | bytes 12288 | tf_op jit(solution)/shard_map/while/body/eval_jaxpr/jit(_take)/gather | solution.py:48
  208.7 3.2 fusion.41
  212.7 5.7 %gather_fusion = f32[1024]{0:T(1024)S(1)} fusion(f32[4096]{0:T(1024)} %get-tuple-element.438, s32[1024]{0:T(1024)S(1)} %get-tuple-element.386), kind=kCustom, calls=%fused_computation.clone.clone.1 | custom fusion | bytes 12288 | tf_op jit(solution)/shard_map/while/body/eval_jaxpr/jit(_take)/gather | solution.py:48
  220.6 3.2 fusion.41
  224.5 5.7 %gather_fusion = f32[1024]{0:T(1024)S(1)} fusion(f32[4096]{0:T(1024)} %get-tuple-element.438, s32[1024]{0:T(1024)S(1)} %get-tuple-element.386), kind=kCustom, calls=%fused_computation.clone.clone.1 | custom fusion | bytes 12288 | tf_op jit(solution)/shard_map/while/body/eval_jaxpr/jit(_take)/gather | solution.py:48
  232.4 3.2 fusion.41
  236.4 5.7 %gather_fusion = f32[1024]{0:T(1024)S(1)} fusion(f32[4096]{0:T(1024)} %get-tuple-element.438, s32[1024]{0:T(1024)S(1)} %get-tuple-element.386), kind=kCustom, calls=%fused_computation.clone.clone.1 | custom fusion | bytes 12288 | tf_op jit(solution)/shard_map/while/body/eval_jaxpr/jit(_take)/gather | solution.py:48
  248.2 5.7 %gather_fusion = f32[1024]{0:T(1024)S(1)} fusion(f32[4096]{0:T(1024)} %get-tuple-element.438, s32[1024]{0:T(1024)S(1)} %get-tuple-element.386), kind=kCustom, calls=%fused_computation.clone.clone.1 | custom fusion | bytes 12288 | tf_op jit(solution)/shard_map/while/body/eval_jaxpr/jit(_take)/gather | solution.py:48
  256.1 3.2 fusion.41
  260.0 5.7 %gather_fusion = f32[1024]{0:T(1024)S(1)} fusion(f32[4096]{0:T(1024)} %get-tuple-element.438, s32[1024]{0:T(1024)S(1)} %get-tuple-element.386), kind=kCustom, calls=%fused_computation.clone.clone.1 | custom fusion | bytes 12288 | tf_op jit(solution)/shard_map/while/body/eval_jaxpr/jit(_take)/gather | solution.py:48
  267.9 3.2 fusion.41
  271.8 5.7 %gather_fusion = f32[1024]{0:T(1024)S(1)} fusion(f32[4096]{0:T(1024)} %get-tuple-element.438, s32[1024]{0:T(1024)S(1)} %get-tuple-element.386), kind=kCustom, calls=%fused_computation.clone.clone.1 | custom fusion | bytes 12288 | tf_op jit(solution)/shard_map/while/body/eval_jaxpr/jit(_take)/gather | solution.py:48
  279.7 3.2 fusion.41
  283.7 5.7 %gather_fusion = f32[1024]{0:T(1024)S(1)} fusion(f32[4096]{0:T(1024)} %get-tuple-element.438, s32[1024]{0:T(1024)S(1)} %get-tuple-element.386), kind=kCustom, calls=%fused_computation.clone.clone.1 | custom fusion | bytes 12288 | tf_op jit(solution)/shard_map/while/body/eval_jaxpr/jit(_take)/gather | solution.py:48
  291.6 3.2 fusion.41
  295.5 5.7 %gather_fusion = f32[1024]{0:T(1024)S(1)} fusion(f32[4096]{0:T(1024)} %get-tuple-element.438, s32[1024]{0:T(1024)S(1)} %get-tuple-element.386), kind=kCustom, calls=%fused_computation.clone.clone.1 | custom fusion | bytes 12288 | tf_op jit(solution)/shard_map/while/body/eval_jaxpr/jit(_take)/gather | solution.py:48
  307.3 5.7 %gather_fusion = f32[1024]{0:T(1024)S(1)} fusion(f32[4096]{0:T(1024)} %get-tuple-element.438, s32[1024]{0:T(1024)S(1)} %get-tuple-element.386), kind=kCustom, calls=%fused_computation.clone.clone.1 | custom fusion | bytes 12288 | tf_op jit(solution)/shard_map/while/body/eval_jaxpr/jit(_take)/gather | solution.py:48
  319.2 5.7 %gather_fusion = f32[1024]{0:T(1024)S(1)} fusion(f32[4096]{0:T(1024)} %get-tuple-element.438, s32[1024]{0:T(1024)S(1)} %get-tuple-element.386), kind=kCustom, calls=%fused_computation.clone.clone.1 | custom fusion | bytes 12288 | tf_op jit(solution)/shard_map/while/body/eval_jaxpr/jit(_take)/gather | solution.py:48
  331.0 5.7 %gather_fusion = f32[1024]{0:T(1024)S(1)} fusion(f32[4096]{0:T(1024)} %get-tuple-element.438, s32[1024]{0:T(1024)S(1)} %get-tuple-element.386), kind=kCustom, calls=%fused_computation.clone.clone.1 | custom fusion | bytes 12288 | tf_op jit(solution)/shard_map/while/body/eval_jaxpr/jit(_take)/gather | solution.py:48
  342.1 16.4 %all_to_all.45 = f32[1,32,128]{2,0,1:T(1,128)S(1)} all-to-all(f32[1,32,128]{2,0,1:T(1,128)S(1)} %bitcast.18), channel_id=1, replica_groups=mesh['filt'=4,'dom'=32] {'dom'}, dimensions={1} | all-to-all | bytes 32768 | tf_op jit(solution)/shard_map/all_to_all | solution.py:66
  358.5 4.1 all-to-all-start
  369.6 4.3 %all-to-all-start.2 = ((f32[128,32,128]{2,0,1:T(8,128)}), f32[128,32,128]{2,0,1:T(8,128)S(1)}, u32[]{:S(2)}, u32[]{:S(2)}) async-start(f32[128,32,128]{2,0,1:T(8,128)} %copy.19), calls=%async_computation.2 | async-start | bytes 4194304 | tf_op jit(solution)/shard_map/all_to_all | solution.py:67
  377.3 37.9 %all-gather = f32[32,1,2]{2,1,0:T(1,128)S(1)} all-gather(f32[1,1,2]{2,1,0:T(1,128)S(1)} %maximum_bitcast_fusion), channel_id=1, replica_groups=mesh['filt'=4,'dom'=32] {'dom'}, dimensions={0}, use_global_device_ids=true | all-gather | bytes 264 | tf_op jit(solution)/shard_map/all_gather | solution.py:15
  (144 shorter events, 125.5 us)
Async XLA Ops:
  342.1 20.5 %copy-start = (f32[128,4096]{1,0:T(8,128)}, f32[128,4096]{1,0:T(8,128)S(1)}, u32[]{:S(2)}) copy-start(f32[128,4096]{1,0:T(8,128)S(1)} %get-tuple-element.239) | copy-start | bytes 6291460
  358.5 11.2 %all-to-all-start = ((f32[1,32,128]{2,0,1:T(1,128)}), f32[1,32,128]{2,0,1:T(1,128)S(1)}, u32[]{:S(2)}, u32[]{:S(2)}) async-start(f32[1,32,128]{2,0,1:T(1,128)} %bitcast), calls=%async_computation | async-start | bytes 32768 | tf_op jit(solution)/shard_map/all_to_all | solution.py:65
  364.6 55.9 %copy-start.1 = (f32[16384]{0:T(1024)S(1)}, f32[16384]{0:T(1024)}, u32[]{:S(2)}) copy-start(f32[16384]{0:T(1024)} %get-tuple-element.446) | copy-start | bytes 196612
  369.6 52.8 %all-to-all-start.2 = ((f32[128,32,128]{2,0,1:T(8,128)}), f32[128,32,128]{2,0,1:T(8,128)S(1)}, u32[]{:S(2)}, u32[]{:S(2)}) async-start(f32[128,32,128]{2,0,1:T(8,128)} %copy.19), calls=%async_computation.2 | async-start | bytes 4194304 | tf_op jit(solution)/shard_map/all_to_all | solution.py:67
where the time goes:
time: 429 us; the launch traced here: 423 us
  other arithmetic  164 us (38%)
  local copies, waits for them, and re-layouts  118 us (28%)
  matrix products  74.2 us (17%)
  blocking collectives  54.2 us (13%)
  starting transfers between devices  8.46 us (2%)
    reduce_max x16, other arithmetic, top_step(): jnp.max(jnp.where(member, row_weights[:, None], floor_value), axis=0)  109 us
    gather x16, local copies, waits for them, and re-layouts, sum_step(): own_top = jnp.take(bin_top, row_bins)  92 us
    dot_general x16, matrix products, sum_step(): jnp.dot(row_states, spread, preferred_element_type=jnp.float32)  51.8 us
    all_gather x1, blocking collectives, rows_first(): out, at, finished = (lax.all_gather(both, axis, axis=0, tiled=True), 0, [])  37.9 us
    dot_general x16, matrix products, sum_step(): jnp.dot(ones_row, spread, preferred_element_type=jnp.float32)[0]  22.5 us
    max x16, other arithmetic, top_step(): jnp.maximum(carry, jnp.max(jnp.where(member, row_weights[:, None], floor_...  20.7 us
    all_to_all x1, blocking collectives, body(): lax.all_to_all(totals[None, :], 'dom', split_axis=1, concat_axis=0, tiled...  16.4 us
    convert_element_type x16, other arithmetic, sum_step(): scaled = jnp.exp(row_weights - own_top).astype(jnp.bfloat16)  11.2 us
  transfers between devices with their start and end apart: 2, of which 1 were waited for; matrix products, arithmetic and copies ran while one was open for 3% of the time, Pallas kernels for 0%

commit v1 on v0

v1 whole, which is shorter than its diff:
```python
import functools
import jax
import jax.numpy as jnp
from jax import lax
from jax.experimental import pallas as pl
from jax.experimental.pallas import tpu as pltpu
from jax.sharding import PartitionSpec as P

BINS = 4096
FLOOR = -10000.0
COUNT = 16384
STATE = 128
HALVES = 2
ROWS = STATE // HALVES
CHUNKS = COUNT // 256


def shuffle(x, sub, lane):
    if sub:
        x = jnp.take_along_axis(x, lax.broadcasted_iota(jnp.int32, (8, 128), 0) ^ sub, axis=0,
                                mode="promise_in_bounds")
    if lane:
        x = jnp.take_along_axis(x, lax.broadcasted_iota(jnp.int32, (8, 128), 1) ^ lane, axis=1,
                                mode="promise_in_bounds")
    return x


def is_high(bit):
    if bit < 7:
        return ((lax.broadcasted_iota(jnp.int32, (8, 128), 0) >> (bit - 4)) & 1) == 1
    return ((lax.broadcasted_iota(jnp.int32, (8, 128), 1) >> (bit - 7)) & 1) == 1


def network():
    steps = []
    for k in range(1, 15):
        steps.append((1 << k) - 1)
        for j in range(k - 2, -1, -1):
            steps.append(1 << j)
    return steps


def swap_step(keys, vals, flip, mark_ref, slot):
    top_bit = flip.bit_length() - 1
    vec, sub, lane = flip & 15, (flip >> 4) & 7, flip >> 7
    keys, vals = list(keys), list(vals)
    if not sub and not lane:
        for r in range(16):
            if (r >> top_bit) & 1:
                continue
            q = r ^ vec
            swap = keys[r] > keys[q]
            mark_ref[slot] = swap.astype(jnp.int32)
            slot += 1
            keys[r], keys[q] = jnp.where(swap, keys[q], keys[r]), jnp.where(swap, keys[r], keys[q])
            vals[r], vals[q] = jnp.where(swap, vals[q], vals[r]), jnp.where(swap, vals[r], vals[q])
        return keys, vals, slot
    high = is_high(top_bit)
    other_keys = [shuffle(x, sub, lane) for x in keys]
    other_vals = [shuffle(x, sub, lane) for x in vals]
    out_keys, out_vals = [], []
    for r in range(16):
        q = r ^ vec
        take = (keys[r] > other_keys[q]) ^ high
        mark_ref[slot] = take.astype(jnp.int32)
        slot += 1
        out_keys.append(jnp.where(take, other_keys[q], keys[r]))
        out_vals.append(jnp.where(take, other_vals[q], vals[r]))
    return out_keys, out_vals, slot


def undo_step(vals, flip, mark_ref, slot):
    top_bit = flip.bit_length() - 1
    vec, sub, lane = flip & 15, (flip >> 4) & 7, flip >> 7
    vals = list(vals)
    if not sub and not lane:
        slot -= 8
        at = slot
        for r in range(16):
            if (r >> top_bit) & 1:
                continue
            q = r ^ vec
            swap = mark_ref[at] != 0
            at += 1
            vals[r], vals[q] = jnp.where(swap, vals[q], vals[r]), jnp.where(swap, vals[r], vals[q])
        return vals, slot
    slot -= 16
    others = [shuffle(x, sub, lane) for x in vals]
    return [jnp.where(mark_ref[slot + r] != 0, others[r ^ vec], vals[r]) for r in range(16)], slot


def rotate(x, by, axis):
    size = x.shape[axis]
    at = (lax.broadcasted_iota(jnp.int32, (8, 128), axis) + by) & (size - 1)
    return jnp.take_along_axis(x, at, axis=axis, mode="promise_in_bounds")


def shifted(vecs, by):
    step = abs(by)
    sign = 1 if by > 0 else -1
    if step >= 128:
        return [rotate(x, by // 128, 1) for x in vecs]
    sublane = lax.broadcasted_iota(jnp.int32, (8, 128), 0)

    def carry_sub(x, m):
        moved = rotate(x, m, 0)
        crossed = rotate(moved, sign, 1)
        inside = (sublane + m < 8) if m > 0 else (sublane + m >= 0)
        return jnp.where(inside, moved, crossed)

    if step >= 16:
        return [carry_sub(x, by // 16) for x in vecs]
    out = []
    for r in range(16):
        q = r + by
        out.append(vecs[q] if 0 <= q < 16 else carry_sub(vecs[q % 16], sign))
    return out


def segment_tops(groups, vals):
    for sign in (1, -1):
        for level in range(14):
            by = sign * (1 << level)
            near_groups, near_vals = shifted(groups, by), shifted(vals, by)
            vals = [
                jnp.where(g == ng, jnp.maximum(v, nv), v)
                for g, ng, v, nv in zip(groups, near_groups, vals, near_vals)
            ]
    return vals


def own_tops(bins_ref, weights_ref, mark_ref):
    lane = lax.broadcasted_iota(jnp.int32, (8, 128), 1)
    sublane = lax.broadcasted_iota(jnp.int32, (8, 128), 0)
    keys, vals = [], []
    for r in range(16):
        rows = pl.ds(8 * r, 8)
        keys.append(bins_ref[rows, :] * COUNT + (lane * 128 + sublane * 16 + r))
        vals.append(weights_ref[rows, :])
    slot = 0
    for flip in network():
        keys, vals, slot = swap_step(keys, vals, flip, mark_ref, slot)
    groups = [k >> 14 for k in keys]
    vals = segment_tops(groups, vals)
    for flip in reversed(network()):
        vals, slot = undo_step(vals, flip, mark_ref, slot)
    return vals


MARKS = sum(8 if flip < 16 else 16 for flip in network())


def rows_of(ref, chunk):
    return jnp.concatenate([ref[pl.ds(2 * chunk, 1), :], ref[pl.ds(2 * chunk + 1, 1), :]], axis=1)


def tile_of(row):
    return jnp.broadcast_to(row, (16, 256)).astype(jnp.bfloat16)


def local_kernel(bins_ref, weights_ref, states_hbm, sums_ref, mass_ref, top_ref, mark_ref,
                 states_ref, iota_ref, key0_ref, key1_ref, part_ref, scaled_ref, flag_ref, t1_ref,
                 t2_ref, t3_ref, copy_sem):
    load = pltpu.make_async_copy(states_hbm, states_ref, copy_sem)
    load.start()
    tops = own_tops(bins_ref, weights_ref, mark_ref)
    for r in range(16):
        rows = pl.ds(8 * r, 8)
        w, b, top = weights_ref[rows, :], bins_ref[rows, :], tops[r]
        flag = w == top
        scaled = jnp.where(flag, 1.0, jnp.exp(w - top))
        scaled_ref[rows, :] = scaled
        low = (b & 255).astype(jnp.float32)
        upper = (b & 256) != 0
        key0_ref[rows, :] = jnp.where(upper, -1.0, low)
        key1_ref[rows, :] = jnp.where(upper, low, -1.0)
        part_ref[rows, :] = (b >> 9).astype(jnp.float32)
        t1 = top.astype(jnp.bfloat16).astype(jnp.float32)
        t2 = (top - t1).astype(jnp.bfloat16).astype(jnp.float32)
        t3 = top - t1 - t2
        flag_ref[rows, :] = jnp.where(flag, 1.0, 0.0)
        t1_ref[rows, :] = jnp.where(flag, t1, 0.0)
        t2_ref[rows, :] = jnp.where(flag, t2, 0.0)
        t3_ref[rows, :] = jnp.where(flag, t3, 0.0)
    iota_ref[...] = lax.broadcasted_iota(jnp.int32, (256, 128), 0).astype(jnp.float32).astype(jnp.bfloat16)
    load.wait()

    def push(chunk, register):
        scaled = tile_of(rows_of(scaled_ref, chunk))
        for q, key_ref in enumerate((key0_ref, key1_ref)):
            key = tile_of(rows_of(key_ref, chunk))
            halves = []
            for side in range(2):
                lanes = slice(128 * side, 128 * side + 128)
                key_full = jnp.concatenate([key[:, lanes]] * 16, axis=0)
                scaled_full = jnp.concatenate([scaled[:, lanes]] * 16, axis=0)
                halves.append(jnp.where(iota_ref[...] == key_full, scaled_full, jnp.bfloat16(0)))
            pltpu.matmul_push_rhs(jnp.concatenate(halves, axis=1), staging_register=register,
                                  mxu_index=q, transpose=True)

    def run(*accs):
        accs = (accs[:9], accs[9:])

        def multiply(chunk, register, half):
            part = tile_of(rows_of(part_ref, chunk))
            cols = pl.ds(pl.multiple_of(chunk * 256, 256), 256)
            block = states_ref[pl.ds(half * ROWS, ROWS), cols]
            for p in range(8):
                mask = jnp.where(part == p, jnp.bfloat16(1), jnp.bfloat16(0))
                lhs = block * jnp.concatenate([mask] * (ROWS // 16), axis=0)
                for q in range(2):
                    pltpu.matmul_acc_lhs(accs[q][p], lhs,
                                         load_staged_rhs=register if p == 0 else None)
            if half == 0:
                row = lax.broadcasted_iota(jnp.int32, (16, 256), 0)
                lower = row < 8
                mine = (row & 7).astype(jnp.float32) == jnp.broadcast_to(rows_of(part_ref, chunk), (16, 256))
                flag, t1, t2, t3 = (
                    jnp.broadcast_to(rows_of(ref, chunk), (16, 256))
                    for ref in (flag_ref, t1_ref, t2_ref, t3_ref)
                )
                groups = (jnp.where(lower, 1.0, flag), jnp.where(lower, t1, t2), jnp.where(lower, t3, 0.0))
                lhs = jnp.concatenate(
                    [jnp.where(mine, g, 0.0).astype(jnp.bfloat16) for g in groups], axis=0)
                for q in range(2):
                    pltpu.matmul_acc_lhs(accs[q][8], lhs)

        for q in range(2):
            for a in accs[q]:
                pltpu.matmul_pop(a)
        push(0, 0)
        for half in range(HALVES):
            @pl.loop(0, CHUNKS, step=2)
            def _(chunk):
                multiply(chunk, 0, half)
                push(chunk + 1, 1)
                multiply(chunk + 1, 1, half)
                push((chunk + 2) & (CHUNKS - 1), 0)

            for p in range(8):
                for q in range(2):
                    sums_ref[ROWS * half:ROWS * half + ROWS, 512 * p + 256 * q:512 * p + 256 * q + 256] = (
                        pltpu.matmul_pop(accs[q][p]))
            if half == 0:
                for q in range(2):
                    extra = pltpu.matmul_pop(accs[q][8])
                    cols = slice(256 * q, 256 * q + 256)
                    mass_ref[:, cols] = extra[0:8]
                    hits = extra[8:16]
                    each = jnp.maximum(hits, 1.0)
                    t1, t2, t3 = (
                        (extra[8 * i:8 * i + 8] / each).astype(jnp.bfloat16).astype(jnp.float32)
                        for i in (2, 3, 4)
                    )
                    top_ref[:, cols] = jnp.where(hits > 0.0, (t1 + t2) + t3, FLOOR)
        for q in range(2):
            pltpu.matmul_acc_lhs(accs[q][8], jnp.zeros((48, 256), jnp.bfloat16), load_staged_rhs=0)
            pltpu.matmul_pop(accs[q][8])

    specs = []
    for q in range(2):
        specs += [pltpu.ACC(q)((ROWS, 256), jnp.float32)] * 8 + [pltpu.ACC(q)((48, 256), jnp.float32)]
    pl.run_scoped(run, *specs)


def local_sums(log_weights, bins, states):
    vmem = pl.BlockSpec(memory_space=pltpu.VMEM)
    table = pltpu.VMEM((128, 128), jnp.float32)
    return pl.pallas_call(
        local_kernel,
        out_shape=(
            jax.ShapeDtypeStruct((STATE, BINS), jnp.float32),
            jax.ShapeDtypeStruct((8, 512), jnp.float32),
            jax.ShapeDtypeStruct((8, 512), jnp.float32),
        ),
        in_specs=[vmem, vmem, pl.BlockSpec(memory_space=pl.ANY)],
        out_specs=(vmem, vmem, vmem),
        scratch_shapes=[
            pltpu.VMEM((MARKS, 8, 128), jnp.int32),
            pltpu.VMEM((STATE, COUNT), jnp.bfloat16),
            pltpu.VMEM((256, 128), jnp.bfloat16),
        ] + [table] * 8 + [pltpu.SemaphoreType.DMA],
        compiler_params=pltpu.CompilerParams(vmem_limit_bytes=40 * 1024 * 1024),
        name="local_sums",
    )(bins.reshape(128, 128), log_weights.reshape(128, 128), states)


def rows_first(arrays, axis, dims):
    turned = [jnp.moveaxis(a, dim, 0) for a, dim in zip(arrays, dims)]
    both = jnp.concatenate([t.reshape(len(t), -1) for t in turned], axis=1)
    out, at, finished = (lax.all_gather(both, axis, axis=0, tiled=True), 0, [])
    for t, dim in zip(turned, dims):
        piece = out[:, at : at + t[0].size].reshape(-1, *t.shape[1:])
        finished.append(jnp.moveaxis(piece, 0, dim))
        at += t[0].size
    return tuple(finished)


def body(log_weights, bins, states):
    groups = lax.axis_size("dom")
    owned = BINS // groups
    sums, totals, bin_top = local_sums(log_weights, bins, states)
    both = jnp.stack([bin_top.reshape(BINS), totals.reshape(BINS)])
    pieces = lax.all_to_all(both, "dom", split_axis=1, concat_axis=0, tiled=True).reshape(groups, 2, owned)
    top_pieces, mass_pieces = pieces[:, 0], pieces[:, 1]
    sum_pieces = lax.all_to_all(sums, "dom", split_axis=1, concat_axis=0, tiled=True)
    sum_pieces = sum_pieces.reshape(groups, sums.shape[0], owned)
    owned_top = jnp.max(top_pieces, axis=0)
    factor = jnp.exp(top_pieces - owned_top[None, :])
    owned_mass = jnp.sum(mass_pieces * factor, axis=0)
    owned_sums = jnp.sum(sum_pieces * factor[:, None, :], axis=0)
    block_top = jnp.max(owned_top)
    block_mass = jnp.sum(owned_mass * jnp.exp(owned_top - block_top))
    all_tops, all_masses = rows_first((block_top[None], block_mass[None]), "dom", (0, 0))
    top = jnp.max(all_tops)
    scaled_masses = all_masses * jnp.exp(all_tops - top)
    total = jnp.sum(scaled_masses)
    lower = lax.iota(jnp.int32, groups) < lax.axis_index("dom")
    before = jnp.sum(jnp.where(lower, scaled_masses, jnp.float32(0.0)))
    share = owned_mass * jnp.exp(owned_top - top)
    cumulative = (before + jnp.cumsum(share)) / total
    bin_means = owned_sums / jnp.maximum(owned_mass, 1.0)[None, :]
    whole_count = log_weights.shape[0] * groups
    particle_weights = whole_count * jnp.exp(log_weights - top) / total
    return (cumulative, bin_means, particle_weights)


def solution(mesh):
    placed = (P(("filt", "dom")), P(("filt", "dom")), P(None, ("filt", "dom")))
    return jax.shard_map(
        body,
        mesh=mesh,
        in_specs=placed,
        out_specs=(P(("filt", "dom")), P(None, ("filt", "dom")), P(("filt", "dom"))),
        check_vma=False,
    )
```

time: 429 us -> 102 us (0.24); the launches traced: 423 us -> 101 us
  other arithmetic: 164 us -> 11.9 us
  local copies, waits for them, and re-layouts: 118 us -> 5.69 us
  matrix products: 74.2 us -> 0 us
  Pallas kernels: 0 us -> 26 us
  blocking collectives: 54.2 us -> 37.9 us
  starting transfers between devices: 8.46 us -> 13.7 us
    reduce_max x16 -> x0, other arithmetic: 109 us -> none  [top_step(): jnp.max(jnp.where(member, row_weights[:, None], floor_value), axis=0)]
    gather x16 -> x0, local copies, waits for them, and re-layouts: 92 us -> none  [sum_step(): own_top = jnp.take(bin_top, row_bins)]
    dot_general x32 -> x0, matrix products: 74.2 us -> none  [the longest x16 51.8 us: sum_step(): jnp.dot(row_states, spread, preferred_element_type=jnp.float32)]
    pallas_call x0 -> x1, Pallas kernels: none -> 26 us  [local_sums(): pl.pallas_call(local_kernel, out_shape=(jax.ShapeDtypeStruct((STATE, BINS...]
    dynamic_slice x32 -> x0, local copies, waits for them, and re-layouts: 22 us -> none  [the longest x16 11 us: top_step(): row_weights = lax.dynamic_slice_in_dim(log_weights, start, width)]
    max x16 -> x0, other arithmetic: 20.7 us -> none  [top_step(): jnp.maximum(carry, jnp.max(jnp.where(member, row_weights[:, None], floor_...]
    all_to_all x1 -> x0, blocking collectives: 16.4 us -> none  [body(): lax.all_to_all(totals[None, :], 'dom', split_axis=1, concat_axis=0, tiled...]
    convert_element_type x16 -> x0, other arithmetic: 11.2 us -> none  [sum_step(): scaled = jnp.exp(row_weights - own_top).astype(jnp.bfloat16)]
  transfers between devices with their start and end apart: 2 -> 2, of which waited for: 1 -> 1; matrix products, arithmetic and copies ran while one was open for 3% -> 12% of each run, Pallas kernels for 0% -> 0%
where the time goes in v1:
time: 102 us; the launch traced here: 101 us
  blocking collectives  37.9 us (37%)
  Pallas kernels  26 us (25%)
  starting transfers between devices  13.7 us (13%)
  other arithmetic  11.9 us (12%)
  local copies, waits for them, and re-layouts  5.69 us (6%)
  waiting for transfers between devices  5.67 us (6%)
    all_gather x1, blocking collectives, rows_first(): out, at, finished = (lax.all_gather(both, axis, axis=0, tiled=True), 0, [])  37.9 us
    pallas_call x1, Pallas kernels, local_sums(): pl.pallas_call(local_kernel, out_shape=(jax.ShapeDtypeStruct((STATE, BINS...  26 us
    all_to_all x1, starting transfers between devices, body(): lax.all_to_all(both, 'dom', split_axis=1, concat_axis=0, tiled=True)  9.59 us
    all_to_all x1, waiting for transfers between devices, body(): lax.all_to_all(both, 'dom', split_axis=1, concat_axis=0, tiled=True)  5.67 us
    all_to_all x1, starting transfers between devices, body(): lax.all_to_all(sums, 'dom', split_axis=1, concat_axis=0, tiled=True)  4.06 us
    unnamed x8, local copies, waits for them, and re-layouts  3.86 us
  transfers between devices with their start and end apart: 2, of which 1 were waited for; matrix products, arithmetic and copies ran while one was open for 12% of the time, Pallas kernels for 0%

profile of v1, /device:TPU:1, one launch (start us, length us, event | category | flops | bytes accessed | tf_op | source)
XLA Modules:
  0.0 101.4 jit_solution(11186057124048503227)
XLA Ops:
  0.6 0.0 copy-start
  0.6 2.2 %copy-done = bf16[128,16384]{1,0:T(8,128)(2,1)S(1)} copy-done((bf16[128,16384]{1,0:T(8,128)(2,1)S(1)}, bf16[128,16384]{1,0:T(8,128)(2,1)}, u32[]{:S(2)}) %copy-start) | copy-done | bytes 4194328
  2.8 0.0 copy-start.1
  2.8 0.8 copy-done.1
  3.7 0.0 copy-start.3
  3.7 0.8 copy-done.3
  4.5 26.0 %local_sums.1 = (f32[128,4096]{1,0:T(8,128)S(1)}, f32[8,512]{1,0:T(8,128)S(1)}, f32[8,512]{1,0:T(8,128)S(1)}) custom-call(s32[128,128]{1,0:T(8,128)S(1)} %bitcast.26, f32[128,128]{1,0:T(8,128)S(1)} %bitcast.25, bf16[128,16384]{1,0:T(8,128)(2,1)S(1)} %copy-done), custom_call_target="tpu_custom_call" | custom-call | tf_op jit(solution)/shard_map/local_sums/pallas_call | solution.py:269
  30.5 0.6 pad_maximum_fusion
  31.2 9.6 %all-to-all-start = ((f32[2,32,128]{2,0,1:T(2,128)}), f32[2,32,128]{2,0,1:T(2,128)S(1)}, u32[]{:S(2)}, u32[]{:S(2)}) async-start(f32[2,32,128]{2,0,1:T(2,128)} %pad_maximum_fusion), calls=%async_computation | async-start | bytes 65536 | tf_op jit(solution)/shard_map/all_to_all | solution.py:304
  40.8 1.6 %copy_bitcast_fusion = f32[128,32,128]{2,0,1:T(8,128)} fusion(f32[128,4096]{1,0:T(8,128)S(1)} %get-tuple-element.8), kind=kLoop, calls=%fused_computation | loop fusion | bytes 4194304 | tf_op jit(solution)/shard_map/all_to_all | solution.py:306
  42.4 0.0 copy-start.2
  42.4 5.7 %all-to-all-done = f32[2,32,128]{2,0,1:T(2,128)S(1)} async-done(((f32[2,32,128]{2,0,1:T(2,128)}), f32[2,32,128]{2,0,1:T(2,128)S(1)}, u32[]{:S(2)}, u32[]{:S(2)}) %all-to-all-start) | async-done | bytes 32800 | tf_op jit(solution)/shard_map/all_to_all | solution.py:304
  48.0 4.1 %all-to-all-start.1 = ((f32[128,32,128]{2,0,1:T(8,128)}), f32[128,32,128]{2,0,1:T(8,128)S(1)}, u32[]{:S(2)}, u32[]{:S(2)}) async-start(f32[128,32,128]{2,0,1:T(8,128)} %copy_bitcast_fusion), calls=%async_computation.1 | async-start | bytes 4194304 | tf_op jit(solution)/shard_map/all_to_all | solution.py:306
  52.2 0.6 fusion.2
  52.8 1.3 %multiply_reduce_fusion.2 = f32[]{:T(128)} fusion(f32[128]{0:T(128)S(1)} %multiply_reduce_fusion.1, f32[128]{0:T(128)S(1)} %get-tuple-element.10, f32[]{:T(128)} %get-tuple-element.9), kind=kLoop, calls=%fused_computation.14 | loop fusion | flops 383 | bytes 1032 | tf_op jit(solution)/shard_map/reduce_sum | solution.py:313
  54.0 1.4 %maximum_bitcast_fusion = f32[1,1,2]{2,1,0:T(1,128)S(1)} fusion(f32[1,1]{1,0:T(1,128)} %bitcast.8, f32[1,1]{1,0:T(1,128)} %bitcast.5), kind=kLoop, calls=%fused_computation.11 | loop fusion | flops 2 | bytes 16
  55.4 37.9 %all-gather = f32[32,1,2]{2,1,0:T(1,128)S(1)} all-gather(f32[1,1,2]{2,1,0:T(1,128)S(1)} %maximum_bitcast_fusion), channel_id=1, replica_groups=mesh['filt'=4,'dom'=32] {'dom'}, dimensions={0}, use_global_device_ids=true | all-gather | bytes 264 | tf_op jit(solution)/shard_map/all_gather | solution.py:291
  93.3 0.1 copy.13
  93.3 0.6 slice_reduce_fusion
  94.0 0.7 broadcast_maximum_fusion
  94.6 0.1 copy.14
  94.7 0.2 reduce-window.9
  94.9 1.3 %fusion.1 = (f32[]{:T(128)}, f32[32,1]{0,1:T(1,128)S(1)}) fusion(s32[]{:T(128)S(6)} %axis_index.12, f32[]{:T(128)} %slice_reduce_fusion, f32[32,2]{0,1:T(2,128)S(1)} %bitcast.35), kind=kLoop, calls=%fused_computation.10 | loop fusion | flops 159 | bytes 396 | tf_op jit(solution)/shard_map/reduce_sum | solution.py:319
  96.1 0.6 reduce_sum.48
  96.8 1.9 %fusion = f32[128]{0:T(128)} fusion(f32[128,1]{1,0:T(8,128)S(1)} %reduce-window.9, f32[]{:T(128)} %reduce_sum.48, f32[]{:T(128)} %get-tuple-element.11), kind=kLoop, calls=%fused_computation.4 | loop fusion | flops 256 | bytes 1032 | tf_op jit(solution)/shard_map/div | solution.py:321
  98.7 0.0 copy-done.2
  98.7 1.9 %multiply_divide_fusion = f32[16384]{0:T(1024)} fusion(f32[16384]{0:T(1024)S(1)} %copy-done.2, f32[]{:T(128)} %reduce_sum.48, f32[]{:T(128)} %slice_reduce_fusion), kind=kLoop, calls=%fused_computation.2 | loop fusion | flops 49152 | bytes 131080 | tf_op jit(solution)/shard_map/div | solution.py:324
  100.6 0.0 all-to-all-done.1
  100.6 0.2 multiply_reduce_fusion
  100.8 0.6 broadcast_divide_fusion
  (5 shorter events, 0.1 us)
Async XLA Ops:
  0.6 2.2 %copy-start = (bf16[128,16384]{1,0:T(8,128)(2,1)S(1)}, bf16[128,16384]{1,0:T(8,128)(2,1)}, u32[]{:S(2)}) copy-start(bf16[128,16384]{1,0:T(8,128)(2,1)} %states_hbm.1) | copy-start | bytes 12582916
  2.8 0.8 copy-start.1
  3.7 0.8 copy-start.3
  31.2 16.9 %all-to-all-start = ((f32[2,32,128]{2,0,1:T(2,128)}), f32[2,32,128]{2,0,1:T(2,128)S(1)}, u32[]{:S(2)}, u32[]{:S(2)}) async-start(f32[2,32,128]{2,0,1:T(2,128)} %pad_maximum_fusion), calls=%async_computation | async-start | bytes 65536 | tf_op jit(solution)/shard_map/all_to_all | solution.py:304
  42.4 56.3 %copy-start.2 = (f32[16384]{0:T(1024)S(1)}, f32[16384]{0:T(1024)}, u32[]{:S(2)}) copy-start(f32[16384]{0:T(1024)} %param.3) | copy-start | bytes 196612
  48.0 52.5 %all-to-all-start.1 = ((f32[128,32,128]{2,0,1:T(8,128)}), f32[128,32,128]{2,0,1:T(8,128)S(1)}, u32[]{:S(2)}, u32[]{:S(2)}) async-start(f32[128,32,128]{2,0,1:T(8,128)} %copy_bitcast_fusion), calls=%async_computation.1 | async-start | bytes 4194304 | tf_op jit(solution)/shard_map/all_to_all | solution.py:306

commit v2 on v1

--- a/solution.py
+++ b/solution.py
@@ -158,7 +158,7 @@
     return jnp.broadcast_to(row, (16, 256)).astype(jnp.bfloat16)
 
 
-def local_kernel(bins_ref, weights_ref, states_hbm, sums_ref, mass_ref, top_ref, mark_ref,
+def local_kernel(bins_ref, weights_ref, states_hbm, sums_ref, tab_ref, mark_ref,
                  states_ref, iota_ref, key0_ref, key1_ref, part_ref, scaled_ref, flag_ref, t1_ref,
                  t2_ref, t3_ref, copy_sem):
     load = pltpu.make_async_copy(states_hbm, states_ref, copy_sem)
@@ -239,20 +239,24 @@
 
             for p in range(8):
                 for q in range(2):
-                    sums_ref[ROWS * half:ROWS * half + ROWS, 512 * p + 256 * q:512 * p + 256 * q + 256] = (
-                        pltpu.matmul_pop(accs[q][p]))
+                    got = pltpu.matmul_pop(accs[q][p])
+                    for side in range(2):
+                        sums_ref[4 * p + 2 * q + side, ROWS * half:ROWS * half + ROWS, :] = (
+                            got[:, 128 * side:128 * side + 128])
             if half == 0:
                 for q in range(2):
                     extra = pltpu.matmul_pop(accs[q][8])
-                    cols = slice(256 * q, 256 * q + 256)
-                    mass_ref[:, cols] = extra[0:8]
                     hits = extra[8:16]
                     each = jnp.maximum(hits, 1.0)
                     t1, t2, t3 = (
                         (extra[8 * i:8 * i + 8] / each).astype(jnp.bfloat16).astype(jnp.float32)
                         for i in (2, 3, 4)
                     )
-                    top_ref[:, cols] = jnp.where(hits > 0.0, (t1 + t2) + t3, FLOOR)
+                    top = jnp.where(hits > 0.0, (t1 + t2) + t3, FLOOR)
+                    for side in range(2):
+                        lanes = slice(128 * side, 128 * side + 128)
+                        tab_ref[pl.ds(2 * q + side, 8, stride=4), :] = top[:, lanes]
+                        tab_ref[pl.ds(32 + 2 * q + side, 8, stride=4), :] = extra[0:8, lanes]
         for q in range(2):
             pltpu.matmul_acc_lhs(accs[q][8], jnp.zeros((48, 256), jnp.bfloat16), load_staged_rhs=0)
             pltpu.matmul_pop(accs[q][8])
@@ -269,12 +273,11 @@
     return pl.pallas_call(
         local_kernel,
         out_shape=(
-            jax.ShapeDtypeStruct((STATE, BINS), jnp.float32),
-            jax.ShapeDtypeStruct((8, 512), jnp.float32),
-            jax.ShapeDtypeStruct((8, 512), jnp.float32),
+            jax.ShapeDtypeStruct((32, STATE, 128), jnp.float32),
+            jax.ShapeDtypeStruct((64, 128), jnp.float32),
         ),
-        in_specs=[vmem, vmem, pl.BlockSpec(memory_space=pl.ANY)],
-        out_specs=(vmem, vmem, vmem),
+        in_specs=[vmem, vmem, pl.BlockSpec(memory_space=pltpu.HBM)],
+        out_specs=(vmem, vmem),
         scratch_shapes=[
             pltpu.VMEM((MARKS, 8, 128), jnp.int32),
             pltpu.VMEM((STATE, COUNT), jnp.bfloat16),
@@ -285,44 +288,166 @@
     )(bins.reshape(128, 128), log_weights.reshape(128, 128), states)
 
 
-def rows_first(arrays, axis, dims):
-    turned = [jnp.moveaxis(a, dim, 0) for a, dim in zip(arrays, dims)]
-    both = jnp.concatenate([t.reshape(len(t), -1) for t in turned], axis=1)
-    out, at, finished = (lax.all_gather(both, axis, axis=0, tiled=True), 0, [])
-    for t, dim in zip(turned, dims):
-        piece = out[:, at : at + t[0].size].reshape(-1, *t.shape[1:])
-        finished.append(jnp.moveaxis(piece, 0, dim))
-        at += t[0].size
-    return tuple(finished)
+CHIPS = 16
+GROUP = 32
+
+
+def hops(off):
+    return sum(min(part, 4 - part) for part in (off >> 2, off & 3))
+
+
+ORDER = sorted(range(1, CHIPS), key=lambda off: (-hops(off), off)) + [0]
+
+
+def lane_sum(row):
+    return jnp.broadcast_to(jnp.sum(row, axis=1, keepdims=True), row.shape)
+
+
+def lane_max(row):
+    return jnp.broadcast_to(jnp.max(row, axis=1, keepdims=True), row.shape)
+
+
+def merge_kernel(whole, sums_ref, tab_ref, weights_ref, cum_ref, means_ref, out_ref,
+                 near_ref, near_tab, fac_ref, mate_ref, merged_ref, note_ref, got_ref, got_note,
+                 word_ref, words_ref,
+                 near_send, near_recv, tab_send, tab_recv, sum_send, sum_recv, note_send, note_recv,
+                 word_send, word_recv):
+    me = lax.axis_index("dom")
+    core = me & 1
+    chip = me >> 1
+    mate = me ^ 1
+
+    def chip_at(off):
+        return ((((chip >> 2) + (off >> 2)) & 3) << 2) | ((chip + (off & 3)) & 3)
+
+    def copy(src, dst, send, recv, target):
+        return pltpu.make_async_remote_copy(
+            src_ref=src, dst_ref=dst, send_sem=send, recv_sem=recv,
+            device_id={"dom": target}, device_id_type=pl.DeviceIdType.MESH)
+
+    barrier = pltpu.get_barrier_semaphore()
+    for i in range(1, GROUP):
+        pl.semaphore_signal(barrier, 1, device_id={"dom": (me + i) & (GROUP - 1)},
+                            device_id_type=pl.DeviceIdType.MESH)
+    pl.semaphore_wait(barrier, GROUP - 1)
+
+    tab_copy = copy(tab_ref, near_tab, tab_send, tab_recv, mate)
+    tab_copy.start()
+    near_copies = []
+    for j, off in enumerate(ORDER):
+        c = copy(sums_ref.at[2 * chip_at(off) + 1 - core], near_ref.at[j], near_send.at[j],
+                 near_recv.at[j], mate)
+        c.start()
+        near_copies.append(c)
+
+    tab_copy.wait()
+    mine = pl.ds(core, CHIPS, stride=2)
+    mine_mass = pl.ds(GROUP + core, CHIPS, stride=2)
+    top_a, top_b = tab_ref[mine, :], near_tab[mine, :]
+    top = jnp.maximum(top_a, top_b)
+    fac_a, fac_b = jnp.exp(top_a - top), jnp.exp(top_b - top)
+    fac_ref[...] = fac_a
+    mate_ref[...] = fac_b
+    note_ref[:, 0, :] = top
+    note_ref[:, 1, :] = tab_ref[mine_mass, :] * fac_a + near_tab[mine_mass, :] * fac_b
+
+    sum_copies, note_copies = [], []
+    for j, off in enumerate(ORDER):
+        where = chip_at(off)
+        near_copies[j].wait()
+        row = pl.ds(where, 1)
+        merged_ref[j] = (sums_ref[2 * where + core] * fac_ref[row, :]
+                         + near_ref[j] * mate_ref[row, :])
+        if off:
+            note = copy(note_ref.at[where], got_note.at[j], note_send.at[j], note_recv.at[j],
+                        2 * where + core)
+            note.start()
+            note_copies.append(note)
+        if j:
+            before = ORDER[j - 1]
+            send = copy(merged_ref.at[j - 1], got_ref.at[j - 1], sum_send.at[j - 1], sum_recv.at[j - 1],
+                        2 * chip_at(before) + core)
+            send.start()
+            sum_copies.append(send)
+
+    got_note[CHIPS - 1] = note_ref[chip]
+    for c in note_copies:
+        c.wait()
+    tops = got_note[:, 0, :]
+    bin_top = jnp.max(tops, axis=0, keepdims=True)
+    factor = jnp.exp(tops - bin_top)
+    bin_mass = jnp.sum(got_note[:, 1, :] * factor, axis=0, keepdims=True)
+    block_top = lane_max(bin_top)
+    word_ref[0:1, :] = block_top
+    word_ref[1:2, :] = lane_sum(bin_mass * jnp.exp(bin_top - block_top))
+    words_ref[0] = word_ref[...]
+    word_copies = []
+    for i in range(1, GROUP):
+        c = copy(word_ref, words_ref.at[i], word_send.at[i], word_recv.at[i], (me + i) & (GROUP - 1))
+        c.start()
+        word_copies.append(c)
+    for c in word_copies:
+        c.wait()
+    all_tops, all_masses = words_ref[:, 0, :], words_ref[:, 1, :]
+    top_all = jnp.max(all_tops, axis=0, keepdims=True)
+    scaled = all_masses * jnp.exp(all_tops - top_all)
+    total = jnp.sum(scaled, axis=0, keepdims=True)
+    at = lax.broadcasted_iota(jnp.int32, (GROUP, 128), 0)
+    lower = (at >= 1) & (at <= me)
+    before = jnp.sum(jnp.where(lower, scaled, 0.0), axis=0, keepdims=True)
+    run = bin_mass * jnp.exp(bin_top - top_all)
+    lane = lax.broadcasted_iota(jnp.int32, (1, 128), 1)
+    for level in range(7):
+        by = 1 << level
+        run = run + jnp.where(lane >= by, pltpu.roll(run, by, 1), 0.0)
+    cum_ref[...] = (before + run) / total
+    out_ref[...] = jnp.exp(weights_ref[...] - top_all) * (whole / total)
+
+    acc = merged_ref[CHIPS - 1] * factor[CHIPS - 1:CHIPS]
+    for j, c in enumerate(sum_copies):
+        c.wait()
+        acc = acc + got_ref[j] * factor[j:j + 1]
+    means_ref[...] = acc / jnp.maximum(bin_mass, 1.0)
+
+
+def merge(sums, tab, log_weights, whole):
+    vmem = pl.BlockSpec(memory_space=pltpu.VMEM)
+    dma = pltpu.SemaphoreType.DMA
+    f32 = jnp.float32
+    return pl.pallas_call(
+        functools.partial(merge_kernel, float(whole)),
+        out_shape=(
+            jax.ShapeDtypeStruct((1, 128), f32),
+            jax.ShapeDtypeStruct((STATE, 128), f32),
+            jax.ShapeDtypeStruct((128, 128), f32),
+        ),
+        in_specs=[vmem] * 3,
+        out_specs=(vmem,) * 3,
+        scratch_shapes=[
+            pltpu.VMEM((CHIPS, STATE, 128), f32),
+            pltpu.VMEM((2 * GROUP, 128), f32),
+            pltpu.VMEM((CHIPS, 128), f32),
+            pltpu.VMEM((CHIPS, 128), f32),
+            pltpu.VMEM((CHIPS, STATE, 128), f32),
+            pltpu.VMEM((CHIPS, 2, 128), f32),
+            pltpu.VMEM((CHIPS, STATE, 128), f32),
+            pltpu.VMEM((CHIPS, 2, 128), f32),
+            pltpu.VMEM((2, 128), f32),
+            pltpu.VMEM((GROUP, 2, 128), f32),
+            dma((CHIPS,)), dma((CHIPS,)), dma, dma, dma((CHIPS,)), dma((CHIPS,)),
+            dma((CHIPS,)), dma((CHIPS,)), dma((GROUP,)), dma((GROUP,)),
+        ],
+        compiler_params=pltpu.CompilerParams(collective_id=0, has_side_effects=True,
+                                             vmem_limit_bytes=24 * 1024 * 1024),
+        name="merge",
+    )(sums, tab, log_weights.reshape(128, 128))
 
 
 def body(log_weights, bins, states):
     groups = lax.axis_size("dom")
-    owned = BINS // groups
-    sums, totals, bin_top = local_sums(log_weights, bins, states)
-    both = jnp.stack([bin_top.reshape(BINS), totals.reshape(BINS)])
-    pieces = lax.all_to_all(both, "dom", split_axis=1, concat_axis=0, tiled=True).reshape(groups, 2, owned)
-    top_pieces, mass_pieces = pieces[:, 0], pieces[:, 1]
-    sum_pieces = lax.all_to_all(sums, "dom", split_axis=1, concat_axis=0, tiled=True)
-    sum_pieces = sum_pieces.reshape(groups, sums.shape[0], owned)
-    owned_top = jnp.max(top_pieces, axis=0)
-    factor = jnp.exp(top_pieces - owned_top[None, :])
-    owned_mass = jnp.sum(mass_pieces * factor, axis=0)
-    owned_sums = jnp.sum(sum_pieces * factor[:, None, :], axis=0)
-    block_top = jnp.max(owned_top)
-    block_mass = jnp.sum(owned_mass * jnp.exp(owned_top - block_top))
-    all_tops, all_masses = rows_first((block_top[None], block_mass[None]), "dom", (0, 0))
-    top = jnp.max(all_tops)
-    scaled_masses = all_masses * jnp.exp(all_tops - top)
-    total = jnp.sum(scaled_masses)
-    lower = lax.iota(jnp.int32, groups) < lax.axis_index("dom")
-    before = jnp.sum(jnp.where(lower, scaled_masses, jnp.float32(0.0)))
-    share = owned_mass * jnp.exp(owned_top - top)
-    cumulative = (before + jnp.cumsum(share)) / total
-    bin_means = owned_sums / jnp.maximum(owned_mass, 1.0)[None, :]
-    whole_count = log_weights.shape[0] * groups
-    particle_weights = whole_count * jnp.exp(log_weights - top) / total
-    return (cumulative, bin_means, particle_weights)
+    sums, tab = local_sums(log_weights, bins, states)
+    cumulative, bin_means, particle_weights = merge(sums, tab, log_weights, log_weights.shape[0] * groups)
+    return cumulative.reshape(128), bin_means, particle_weights.reshape(COUNT)
 
 
 def solution(mesh):

time: 102 us -> 61.3 us (0.60)
  blocking collectives: 37.9 us -> 0 us
  Pallas kernels: 26 us -> 54.8 us
  starting transfers between devices: 13.7 us -> 0 us
  other arithmetic: 11.9 us -> 0 us
  waiting for transfers between devices: 5.67 us -> 0 us
    all_gather x1 -> x0, blocking collectives: 37.9 us -> none  [rows_first(): out, at, finished = (lax.all_gather(both, axis, axis=0, tiled=True), 0, [])]
    pallas_call x1 -> x2, Pallas kernels: 26 us -> 54.8 us  [the longest x1 28.8 us: merge(): pl.pallas_call(functools.partial(merge_kernel, float(whole)), out_shape=(...]
    all_to_all x2 -> x0, starting transfers between devices: 13.7 us -> none  [the longest x1 9.59 us: body(): lax.all_to_all(both, 'dom', split_axis=1, concat_axis=0, tiled=True)]
    all_to_all x2 -> x0, waiting for transfers between devices: 5.67 us -> none  [the longest x1 5.67 us: body(): lax.all_to_all(both, 'dom', split_axis=1, concat_axis=0, tiled=True)]
    div x3 -> x0, other arithmetic: 4.45 us -> none  [the longest x1 1.91 us: body(): particle_weights = whole_count * jnp.exp(log_weights - top) / total]
    reduce_sum x5 -> x0, other arithmetic: 3.37 us -> none  [the longest x1 1.25 us: body(): block_mass = jnp.sum(owned_mass * jnp.exp(owned_top - block_top))]
    unnamed x8 -> x9, local copies, waits for them, and re-layouts: 3.86 us -> 5.63 us
    all_to_all x1 -> x0, local copies, waits for them, and re-layouts: 1.61 us -> none  [body(): lax.all_to_all(sums, 'dom', split_axis=1, concat_axis=0, tiled=True)]
  transfers between devices with their start and end apart: 2 -> 0, of which waited for: 1 -> 0; matrix products, arithmetic and copies ran while one was open for 12% -> 0% of each run, Pallas kernels for 0% -> 0%
where the time goes in v2:
time: 61.3 us; the launch traced here: 61.1 us
  Pallas kernels  54.8 us (89%)
  local copies, waits for them, and re-layouts  5.63 us (9%)
  between operations  0.66 us (1%)
    pallas_call x1, Pallas kernels, merge(): pl.pallas_call(functools.partial(merge_kernel, float(whole)), out_shape=(...  28.8 us
    pallas_call x1, Pallas kernels, local_sums(): pl.pallas_call(local_kernel, out_shape=(jax.ShapeDtypeStruct((32, STATE,...  26 us
    unnamed x9, local copies, waits for them, and re-layouts  5.63 us

profile of v2, /device:TPU:1, one launch (start us, length us, event | category | flops | bytes accessed | tf_op | source)
XLA Modules:
  0.0 61.1 jit_solution(9150763049069118786)
XLA Ops:
  0.6 0.0 copy-start
  0.6 2.2 %copy-done = bf16[128,16384]{1,0:T(8,128)(2,1)S(1)} copy-done((bf16[128,16384]{1,0:T(8,128)(2,1)S(1)}, bf16[128,16384]{1,0:T(8,128)(2,1)}, u32[]{:S(2)}) %copy-start) | copy-done | bytes 4194328
  2.8 0.0 copy-start.1
  2.8 0.8 %copy-done.1 = f32[16384]{0:T(1024)S(1)} copy-done((f32[16384]{0:T(1024)S(1)}, f32[16384]{0:T(1024)}, u32[]{:S(2)}) %copy-start.1) | copy-done | bytes 65560
  3.7 0.0 copy-start.2
  3.7 0.8 %copy-done.2 = s32[16384]{0:T(1024)S(1)} copy-done((s32[16384]{0:T(1024)S(1)}, s32[16384]{0:T(1024)}, u32[]{:S(2)}) %copy-start.2) | copy-done | bytes 65560
  4.5 26.0 %local_sums.1 = (f32[32,128,128]{2,1,0:T(8,128)S(1)}, f32[64,128]{1,0:T(8,128)S(1)}) custom-call(s32[128,128]{1,0:T(8,128)S(1)} %bitcast.6, f32[128,128]{1,0:T(8,128)S(1)} %bitcast.4, bf16[128,16384]{1,0:T(8,128)(2,1)S(1)} %copy-done), custom_call_target="tpu_custom_call" | custom-call | tf_op jit(solution)/shard_map/local_sums/pallas_call | solution.py:273
  30.5 28.8 %merge.1 = (f32[1,128]{1,0:T(1,128)S(1)}, f32[128,128]{1,0:T(8,128)S(1)}, f32[128,128]{1,0:T(8,128)S(1)}) custom-call(f32[32,128,128]{2,1,0:T(8,128)S(1)} %get-tuple-element.8.sums_ref, f32[64,128]{1,0:T(8,128)S(1)} %get-tuple-element.9.tab_ref, f32[128,128]{1,0:T(8,128)S(1)} %bitcast.5), custom_call_target="tpu_custom_call" | custom-call | tf_op jit(solution)/shard_map/merge/pallas_call | solution.py:417
  59.3 0.5 copy.9
  59.8 0.6 %copy.10 = f32[128,128]{1,0:T(8,128)} copy(f32[128,128]{1,0:T(8,128)S(1)} %get-tuple-element.17) | data formatting | bytes 131072
  60.4 0.6 %copy.11 = f32[16384]{0:T(1024)} copy(f32[16384]{0:T(1024)S(1)} %bitcast.7) | data formatting | bytes 131072
Async XLA Ops:
  0.6 2.2 %copy-start = (bf16[128,16384]{1,0:T(8,128)(2,1)S(1)}, bf16[128,16384]{1,0:T(8,128)(2,1)}, u32[]{:S(2)}) copy-start(bf16[128,16384]{1,0:T(8,128)(2,1)} %states_hbm.1) | copy-start | bytes 12582916
  2.8 0.8 %copy-start.1 = (f32[16384]{0:T(1024)S(1)}, f32[16384]{0:T(1024)}, u32[]{:S(2)}) copy-start(f32[16384]{0:T(1024)} %param.3) | copy-start | bytes 196612
  3.7 0.8 %copy-start.2 = (s32[16384]{0:T(1024)S(1)}, s32[16384]{0:T(1024)}, u32[]{:S(2)}) copy-start(s32[16384]{0:T(1024)} %param.4) | copy-start | bytes 196612

commit v3 on v1

v3 whole, which is shorter than its diff:
```python
import functools
import jax
import jax.numpy as jnp
from jax import lax
from jax.experimental import pallas as pl
from jax.experimental.pallas import tpu as pltpu
from jax.sharding import PartitionSpec as P

BINS = 4096
FLOOR = -10000.0
COUNT = 16384
STATE = 128
GRAIN = 32
PHASES = (64, 32, 32)
CHIPS = 16
GROUP = 32
CHUNKS = COUNT // 256


def shuffle(x, sub, lane):
    if sub:
        x = jnp.take_along_axis(x, lax.broadcasted_iota(jnp.int32, (8, 128), 0) ^ sub, axis=0,
                                mode="promise_in_bounds")
    if lane:
        x = jnp.take_along_axis(x, lax.broadcasted_iota(jnp.int32, (8, 128), 1) ^ lane, axis=1,
                                mode="promise_in_bounds")
    return x


def is_high(bit):
    if bit < 7:
        return ((lax.broadcasted_iota(jnp.int32, (8, 128), 0) >> (bit - 4)) & 1) == 1
    return ((lax.broadcasted_iota(jnp.int32, (8, 128), 1) >> (bit - 7)) & 1) == 1


def network():
    steps = []
    for k in range(1, 15):
        steps.append((1 << k) - 1)
        for j in range(k - 2, -1, -1):
            steps.append(1 << j)
    return steps


def swap_step(keys, vals, flip, mark_ref, slot):
    top_bit = flip.bit_length() - 1
    vec, sub, lane = flip & 15, (flip >> 4) & 7, flip >> 7
    keys, vals = list(keys), list(vals)
    if not sub and not lane:
        for r in range(16):
            if (r >> top_bit) & 1:
                continue
            q = r ^ vec
            swap = keys[r] > keys[q]
            mark_ref[slot] = swap.astype(jnp.int32)
            slot += 1
            keys[r], keys[q] = jnp.where(swap, keys[q], keys[r]), jnp.where(swap, keys[r], keys[q])
            vals[r], vals[q] = jnp.where(swap, vals[q], vals[r]), jnp.where(swap, vals[r], vals[q])
        return keys, vals, slot
    high = is_high(top_bit)
    other_keys = [shuffle(x, sub, lane) for x in keys]
    other_vals = [shuffle(x, sub, lane) for x in vals]
    out_keys, out_vals = [], []
    for r in range(16):
        q = r ^ vec
        take = (keys[r] > other_keys[q]) ^ high
        mark_ref[slot] = take.astype(jnp.int32)
        slot += 1
        out_keys.append(jnp.where(take, other_keys[q], keys[r]))
        out_vals.append(jnp.where(take, other_vals[q], vals[r]))
    return out_keys, out_vals, slot


def undo_step(vals, flip, mark_ref, slot):
    top_bit = flip.bit_length() - 1
    vec, sub, lane = flip & 15, (flip >> 4) & 7, flip >> 7
    vals = list(vals)
    if not sub and not lane:
        slot -= 8
        at = slot
        for r in range(16):
            if (r >> top_bit) & 1:
                continue
            q = r ^ vec
            swap = mark_ref[at] != 0
            at += 1
            vals[r], vals[q] = jnp.where(swap, vals[q], vals[r]), jnp.where(swap, vals[r], vals[q])
        return vals, slot
    slot -= 16
    others = [shuffle(x, sub, lane) for x in vals]
    return [jnp.where(mark_ref[slot + r] != 0, others[r ^ vec], vals[r]) for r in range(16)], slot


def rotate(x, by, axis):
    size = x.shape[axis]
    at = (lax.broadcasted_iota(jnp.int32, (8, 128), axis) + by) & (size - 1)
    return jnp.take_along_axis(x, at, axis=axis, mode="promise_in_bounds")


def shifted(vecs, by):
    step = abs(by)
    sign = 1 if by > 0 else -1
    if step >= 128:
        return [rotate(x, by // 128, 1) for x in vecs]
    sublane = lax.broadcasted_iota(jnp.int32, (8, 128), 0)

    def carry_sub(x, m):
        moved = rotate(x, m, 0)
        crossed = rotate(moved, sign, 1)
        inside = (sublane + m < 8) if m > 0 else (sublane + m >= 0)
        return jnp.where(inside, moved, crossed)

    if step >= 16:
        return [carry_sub(x, by // 16) for x in vecs]
    out = []
    for r in range(16):
        q = r + by
        out.append(vecs[q] if 0 <= q < 16 else carry_sub(vecs[q % 16], sign))
    return out


def segment_tops(groups, vals):
    for sign in (1, -1):
        for level in range(14):
            by = sign * (1 << level)
            near_groups, near_vals = shifted(groups, by), shifted(vals, by)
            vals = [
                jnp.where(g == ng, jnp.maximum(v, nv), v)
                for g, ng, v, nv in zip(groups, near_groups, vals, near_vals)
            ]
    return vals


def own_tops(bins_ref, weights_ref, mark_ref):
    lane = lax.broadcasted_iota(jnp.int32, (8, 128), 1)
    sublane = lax.broadcasted_iota(jnp.int32, (8, 128), 0)
    keys, vals = [], []
    for r in range(16):
        rows = pl.ds(8 * r, 8)
        keys.append(bins_ref[rows, :] * COUNT + (lane * 128 + sublane * 16 + r))
        vals.append(weights_ref[rows, :])
    slot = 0
    for flip in network():
        keys, vals, slot = swap_step(keys, vals, flip, mark_ref, slot)
    groups = [k >> 14 for k in keys]
    vals = segment_tops(groups, vals)
    for flip in reversed(network()):
        vals, slot = undo_step(vals, flip, mark_ref, slot)
    return vals


MARKS = sum(8 if flip < 16 else 16 for flip in network())


def rows_of(ref, chunk):
    return jnp.concatenate([ref[pl.ds(2 * chunk, 1), :], ref[pl.ds(2 * chunk + 1, 1), :]], axis=1)


def tile_of(row):
    return jnp.broadcast_to(row, (16, 256)).astype(jnp.bfloat16)


def hops(off):
    return sum(min(part, 4 - part) for part in (off >> 2, off & 3))


ORDER = sorted(range(1, CHIPS), key=lambda off: (-hops(off), off))


def lane_sum(row):
    return jnp.broadcast_to(jnp.sum(row, axis=1, keepdims=True), row.shape)


def lane_max(row):
    return jnp.broadcast_to(jnp.max(row, axis=1, keepdims=True), row.shape)


def kernel(whole, bins_hbm, weights_hbm, states_hbm, cum_ref, means_ref, out_ref, refs):
    me = lax.axis_index("dom")
    core = me & 1
    chip = me >> 1
    mate = me ^ 1
    bins_ref, weights_ref, states_ref = refs["bins"], refs["weights"], refs["states"]
    tab_ref, near_tab, note_ref, got_note = refs["tab"], refs["near_tab"], refs["note"], refs["got_note"]
    word_ref, words_ref = refs["word"], refs["words"]

    def chip_at(off):
        return ((((chip >> 2) + (off >> 2)) & 3) << 2) | ((chip + (off & 3)) & 3)

    def copy(src, dst, send, recv, target):
        return pltpu.make_async_remote_copy(
            src_ref=src, dst_ref=dst, send_sem=send, recv_sem=recv,
            device_id={"dom": target}, device_id_type=pl.DeviceIdType.MESH)

    loads = [pltpu.make_async_copy(src, dst, refs["load_sem"].at[i]) for i, (src, dst) in enumerate(
        ((bins_hbm, bins_ref), (weights_hbm, weights_ref), (states_hbm, states_ref)))]
    for load in loads:
        load.start()
    barrier = pltpu.get_barrier_semaphore()
    for i in range(1, GROUP):
        pl.semaphore_signal(barrier, 1, device_id={"dom": (me + i) & (GROUP - 1)},
                            device_id_type=pl.DeviceIdType.MESH)
    loads[0].wait()
    loads[1].wait()

    tops = own_tops(bins_ref, weights_ref, refs["marks"])
    for r in range(16):
        rows = pl.ds(8 * r, 8)
        w, b, top = weights_ref[rows, :], bins_ref[rows, :], tops[r]
        flag = w == top
        refs["scaled"][rows, :] = jnp.where(flag, 1.0, jnp.exp(w - top))
        low = (b & 255).astype(jnp.float32)
        upper = (b & 256) != 0
        refs["key0"][rows, :] = jnp.where(upper, -1.0, low)
        refs["key1"][rows, :] = jnp.where(upper, low, -1.0)
        refs["part"][rows, :] = (b >> 9).astype(jnp.float32)
        t1 = top.astype(jnp.bfloat16).astype(jnp.float32)
        t2 = (top - t1).astype(jnp.bfloat16).astype(jnp.float32)
        t3 = top - t1 - t2
        refs["flag"][rows, :] = jnp.where(flag, 1.0, 0.0)
        refs["t1"][rows, :] = jnp.where(flag, t1, 0.0)
        refs["t2"][rows, :] = jnp.where(flag, t2, 0.0)
        refs["t3"][rows, :] = jnp.where(flag, t3, 0.0)
    iota_ref = refs["iota"]
    iota_ref[...] = lax.broadcasted_iota(jnp.int32, (256, 128), 0).astype(jnp.float32).astype(jnp.bfloat16)
    loads[2].wait()
    pl.semaphore_wait(barrier, GROUP - 1)

    def push(chunk, register):
        scaled = tile_of(rows_of(refs["scaled"], chunk))
        for q in range(2):
            key = tile_of(rows_of(refs["key%d" % q], chunk))
            halves = []
            for side in range(2):
                lanes = slice(128 * side, 128 * side + 128)
                key_full = jnp.concatenate([key[:, lanes]] * 16, axis=0)
                scaled_full = jnp.concatenate([scaled[:, lanes]] * 16, axis=0)
                halves.append(jnp.where(iota_ref[...] == key_full, scaled_full, jnp.bfloat16(0)))
            pltpu.matmul_push_rhs(jnp.concatenate(halves, axis=1), staging_register=register,
                                  mxu_index=q, transpose=True)

    near_copies, tab_copy = [], []

    def send_near(h):
        c = copy(refs["sums%d" % h].at[:, 1 - core], refs["near%d" % h], refs["near_send"].at[h],
                 refs["near_recv"].at[h], mate)
        c.start()
        near_copies.append(c)

    def send_tab():
        c = copy(tab_ref, near_tab, refs["tab_send"], refs["tab_recv"], mate)
        c.start()
        tab_copy.append(c)

    sum_copies, note_copies, word_copies = [], [], []

    def join(h):
        near_copies[h].wait()
        sums, near, merged = refs["sums%d" % h], refs["near%d" % h], refs["merged%d" % h]
        for c in range(CHIPS):
            merged[c] = (sums[c, core] * refs["fac"][c:c + 1, :] + near[c] * refs["mate"][c:c + 1, :])

    def send_sums(h):
        sent = []
        for j, off in enumerate(ORDER):
            where = chip_at(off)
            c = copy(refs["merged%d" % h].at[where], refs["got%d" % h].at[j], refs["sum_send%d" % h].at[j],
                     refs["sum_recv%d" % h].at[j], 2 * where + core)
            c.start()
            sent.append(c)
        sum_copies.append(sent)

    def join_tops():
        tab_copy[0].wait()
        mine = pl.ds(core, CHIPS, stride=2)
        mine_mass = pl.ds(GROUP + core, CHIPS, stride=2)
        top_a, top_b = tab_ref[mine, :], near_tab[mine, :]
        top = jnp.maximum(top_a, top_b)
        fac_a, fac_b = jnp.exp(top_a - top), jnp.exp(top_b - top)
        refs["fac"][...] = fac_a
        refs["mate"][...] = fac_b
        note_ref[:, 0, :] = top
        note_ref[:, 1, :] = tab_ref[mine_mass, :] * fac_a + near_tab[mine_mass, :] * fac_b

    def send_notes():
        for j, off in enumerate(ORDER):
            where = chip_at(off)
            c = copy(note_ref.at[where], got_note.at[j], refs["note_send"].at[j], refs["note_recv"].at[j],
                     2 * where + core)
            c.start()
            note_copies.append(c)
        got_note[CHIPS - 1] = note_ref[chip]

    def join_notes():
        for c in note_copies:
            c.wait()
        tops = got_note[:, 0, :]
        bin_top = jnp.max(tops, axis=0, keepdims=True)
        factor = jnp.exp(tops - bin_top)
        bin_mass = jnp.sum(got_note[:, 1, :] * factor, axis=0, keepdims=True)
        refs["factor"][...] = factor
        refs["owned"][0:1, :] = bin_top
        refs["owned"][1:2, :] = bin_mass
        block_top = lane_max(bin_top)
        word_ref[0:1, :] = block_top
        word_ref[1:2, :] = lane_sum(bin_mass * jnp.exp(bin_top - block_top))
        words_ref[0] = word_ref[...]

    def send_words():
        for i in range(1, GROUP):
            c = copy(word_ref, words_ref.at[i], refs["word_send"].at[i], refs["word_recv"].at[i],
                     (me + i) & (GROUP - 1))
            c.start()
            word_copies.append(c)

    def join_words():
        for c in word_copies:
            c.wait()
        all_tops, all_masses = words_ref[:, 0, :], words_ref[:, 1, :]
        top_all = jnp.max(all_tops, axis=0, keepdims=True)
        scaled = all_masses * jnp.exp(all_tops - top_all)
        total = jnp.sum(scaled, axis=0, keepdims=True)
        at = lax.broadcasted_iota(jnp.int32, (GROUP, 128), 0)
        before = jnp.sum(jnp.where((at >= 1) & (at <= me), scaled, 0.0), axis=0, keepdims=True)
        run = refs["owned"][1:2, :] * jnp.exp(refs["owned"][0:1, :] - top_all)
        lane = lax.broadcasted_iota(jnp.int32, (1, 128), 1)
        for level in range(7):
            by = 1 << level
            run = run + jnp.where(lane >= by, pltpu.roll(run, by, 1), 0.0)
        cum_ref[...] = (before + run) / total
        out_ref[...] = jnp.exp(weights_ref[...] - top_all) * (whole / total)

    def gather_sums(h, start):
        acc = refs["merged%d" % h][chip] * refs["factor"][CHIPS - 1:CHIPS, :]
        for j, c in enumerate(sum_copies[h]):
            c.wait()
            acc = acc + refs["got%d" % h][j] * refs["factor"][j:j + 1, :]
        means_ref[start:start + PHASES[h], :] = acc / jnp.maximum(refs["owned"][1:2, :], 1.0)

    most = max(PHASES) // GRAIN

    def run(*accs):
        size = 8 * most + 1
        accs = (accs[:size], accs[size:])

        def multiply(chunk, register, h):
            part = tile_of(rows_of(refs["part"], chunk))
            cols = pl.ds(pl.multiple_of(chunk * 256, 256), 256)
            first = register
            for g in range(PHASES[h] // GRAIN):
                block = states_ref[pl.ds(sum(PHASES[:h]) + g * GRAIN, GRAIN), cols]
                for p in range(8):
                    mask = jnp.where(part == p, jnp.bfloat16(1), jnp.bfloat16(0))
                    lhs = block * jnp.concatenate([mask] * (GRAIN // 16), axis=0)
                    for q in range(2):
                        pltpu.matmul_acc_lhs(accs[q][g * 8 + p], lhs, load_staged_rhs=first)
                    first = None
            if h == 0:
                row = lax.broadcasted_iota(jnp.int32, (16, 256), 0)
                lower = row < 8
                mine = (row & 7).astype(jnp.float32) == jnp.broadcast_to(rows_of(refs["part"], chunk), (16, 256))
                flag, t1, t2, t3 = (
                    jnp.broadcast_to(rows_of(refs[name], chunk), (16, 256))
                    for name in ("flag", "t1", "t2", "t3")
                )
                groups = (jnp.where(lower, 1.0, flag), jnp.where(lower, t1, t2), jnp.where(lower, t3, 0.0))
                lhs = jnp.concatenate(
                    [jnp.where(mine, g, 0.0).astype(jnp.bfloat16) for g in groups], axis=0)
                for q in range(2):
                    pltpu.matmul_acc_lhs(accs[q][size - 1], lhs)

        def chunks(h, start, stop):
            @pl.loop(start, stop, step=2)
            def _(chunk):
                multiply(chunk, 0, h)
                push(chunk + 1, 1)
                multiply(chunk + 1, 1, h)
                push((chunk + 2) & (CHUNKS - 1), 0)

        def drain(h):
            for g in range(PHASES[h] // GRAIN):
                for p in range(8):
                    for q in range(2):
                        got = pltpu.matmul_pop(accs[q][g * 8 + p])
                        for side in range(2):
                            refs["sums%d" % h][2 * p + q, side, GRAIN * g:GRAIN * g + GRAIN, :] = (
                                got[:, 128 * side:128 * side + 128])

        def drain_tops():
            for q in range(2):
                extra = pltpu.matmul_pop(accs[q][size - 1])
                hits = extra[8:16]
                each = jnp.maximum(hits, 1.0)
                t1, t2, t3 = (
                    (extra[8 * i:8 * i + 8] / each).astype(jnp.bfloat16).astype(jnp.float32)
                    for i in (2, 3, 4)
                )
                top = jnp.where(hits > 0.0, (t1 + t2) + t3, FLOOR)
                for side in range(2):
                    lanes = slice(128 * side, 128 * side + 128)
                    tab_ref[pl.ds(2 * q + side, 8, stride=4), :] = top[:, lanes]
                    tab_ref[pl.ds(GROUP + 2 * q + side, 8, stride=4), :] = extra[0:8, lanes]

        for q in range(2):
            for a in accs[q]:
                pltpu.matmul_pop(a)
        push(0, 0)
        chunks(0, 0, CHUNKS)
        drain_tops()
        drain(0)
        send_tab()
        send_near(0)
        chunks(1, 0, SPLIT[0])
        join_tops()
        join(0)
        send_notes()
        send_sums(0)
        chunks(1, SPLIT[0], CHUNKS)
        drain(1)
        send_near(1)
        chunks(2, 0, SPLIT[1])
        join(1)
        join_notes()
        send_sums(1)
        send_words()
        chunks(2, SPLIT[1], CHUNKS)
        drain(2)
        for q in range(2):
            pltpu.matmul_acc_lhs(accs[q][size - 1], jnp.zeros((48, 256), jnp.bfloat16), load_staged_rhs=0)
            pltpu.matmul_pop(accs[q][size - 1])
        send_near(2)
        join_words()
        join(2)
        gather_sums(0, 0)
        send_sums(2)
        gather_sums(1, PHASES[0])
        gather_sums(2, PHASES[0] + PHASES[1])

    specs = []
    for q in range(2):
        specs += [pltpu.ACC(q)((GRAIN, 256), jnp.float32)] * (8 * most) + [pltpu.ACC(q)((48, 256), jnp.float32)]
    pl.run_scoped(run, *specs)


SPLIT = (32, 32)
VMEM_LIMIT = 67043328


def scratch():
    f32, bf16, dma = jnp.float32, jnp.bfloat16, pltpu.SemaphoreType.DMA
    table = pltpu.VMEM((128, 128), f32)
    shapes = dict(
        bins=pltpu.VMEM((128, 128), jnp.int32), weights=table,
        states=pltpu.VMEM((STATE, COUNT), bf16), marks=pltpu.VMEM((MARKS, 8, 128), jnp.int32),
        iota=pltpu.VMEM((256, 128), bf16), scaled=table, key0=table, key1=table, part=table,
        flag=table, t1=table, t2=table, t3=table,
        tab=pltpu.VMEM((2 * GROUP, 128), f32), near_tab=pltpu.VMEM((2 * GROUP, 128), f32),
        fac=pltpu.VMEM((CHIPS, 128), f32), mate=pltpu.VMEM((CHIPS, 128), f32),
        factor=pltpu.VMEM((CHIPS, 128), f32), owned=pltpu.VMEM((2, 128), f32),
        note=pltpu.VMEM((CHIPS, 2, 128), f32), got_note=pltpu.VMEM((CHIPS, 2, 128), f32),
        word=pltpu.VMEM((2, 128), f32), words=pltpu.VMEM((GROUP, 2, 128), f32),
        load_sem=dma((3,)), near_send=dma((len(PHASES),)), near_recv=dma((len(PHASES),)),
        tab_send=dma, tab_recv=dma, note_send=dma((CHIPS,)), note_recv=dma((CHIPS,)),
        word_send=dma((GROUP,)), word_recv=dma((GROUP,)),
    )
    for h, rows in enumerate(PHASES):
        shapes["sums%d" % h] = pltpu.VMEM((CHIPS, 2, rows, 128), f32)
        for name in ("near", "merged", "got"):
            shapes["%s%d" % (name, h)] = pltpu.VMEM((CHIPS, rows, 128), f32)
        shapes["sum_send%d" % h] = dma((CHIPS,))
        shapes["sum_recv%d" % h] = dma((CHIPS,))
    return shapes


def body(log_weights, bins, states):
    whole = log_weights.shape[0] * lax.axis_size("dom")
    vmem = pl.BlockSpec(memory_space=pltpu.VMEM)
    shapes = scratch()

    def call(*args):
        kernel(float(whole), *args[:6], dict(zip(shapes, args[6:])))

    cumulative, bin_means, particle_weights = pl.pallas_call(
        call,
        out_shape=(
            jax.ShapeDtypeStruct((1, 128), jnp.float32),
            jax.ShapeDtypeStruct((STATE, 128), jnp.float32),
            jax.ShapeDtypeStruct((128, 128), jnp.float32),
        ),
        in_specs=[pl.BlockSpec(memory_space=pltpu.HBM)] * 3,
        out_specs=(vmem,) * 3,
        scratch_shapes=list(shapes.values()),
        compiler_params=pltpu.CompilerParams(collective_id=0, has_side_effects=True,
                                             vmem_limit_bytes=VMEM_LIMIT),
        name="resample",
    )(bins.reshape(128, 128), log_weights.reshape(128, 128), states)
    return cumulative.reshape(128), bin_means, particle_weights.reshape(COUNT)


def solution(mesh):
    placed = (P(("filt", "dom")), P(("filt", "dom")), P(None, ("filt", "dom")))
    return jax.shard_map(
        body,
        mesh=mesh,
        in_specs=placed,
        out_specs=(P(("filt", "dom")), P(None, ("filt", "dom")), P(("filt", "dom"))),
        check_vma=False,
    )
```

time: 102 us -> 50 us (0.49)
  blocking collectives: 37.9 us -> 0 us
  Pallas kernels: 26 us -> 44.9 us
  starting transfers between devices: 13.7 us -> 0 us
  other arithmetic: 11.9 us -> 0 us
  waiting for transfers between devices: 5.67 us -> 0 us
  local copies, waits for them, and re-layouts: 5.69 us -> 4.12 us
    all_gather x1 -> x0, blocking collectives: 37.9 us -> none  [rows_first(): out, at, finished = (lax.all_gather(both, axis, axis=0, tiled=True), 0, [])]
    pallas_call x1, Pallas kernels: 26 us -> 44.9 us  [body(): pl.pallas_call(call, out_shape=(jax.ShapeDtypeStruct((1, 128), jnp.float3...]
    all_to_all x2 -> x0, starting transfers between devices: 13.7 us -> none  [the longest x1 9.59 us: body(): lax.all_to_all(both, 'dom', split_axis=1, concat_axis=0, tiled=True)]
    all_to_all x2 -> x0, waiting for transfers between devices: 5.67 us -> none  [the longest x1 5.67 us: body(): lax.all_to_all(both, 'dom', split_axis=1, concat_axis=0, tiled=True)]
    div x3 -> x0, other arithmetic: 4.45 us -> none  [the longest x1 1.91 us: body(): particle_weights = whole_count * jnp.exp(log_weights - top) / total]
    reduce_sum x5 -> x0, other arithmetic: 3.37 us -> none  [the longest x1 1.25 us: body(): block_mass = jnp.sum(owned_mass * jnp.exp(owned_top - block_top))]
    all_to_all x1 -> x0, local copies, waits for them, and re-layouts: 1.61 us -> none  [body(): lax.all_to_all(sums, 'dom', split_axis=1, concat_axis=0, tiled=True)]
    unnamed x1 -> x0, other arithmetic: 1.36 us -> none
  transfers between devices with their start and end apart: 2 -> 0, of which waited for: 1 -> 0; matrix products, arithmetic and copies ran while one was open for 12% -> 0% of each run, Pallas kernels for 0% -> 0%
where the time goes in v3:
time: 50 us; the launch traced here: 49.6 us
  Pallas kernels  44.9 us (90%)
  local copies, waits for them, and re-layouts  4.12 us (8%)
  between operations  0.64 us (1%)
    pallas_call x1, Pallas kernels, body(): pl.pallas_call(call, out_shape=(jax.ShapeDtypeStruct((1, 128), jnp.float3...  44.9 us
    unnamed x3, local copies, waits for them, and re-layouts  4.12 us

profile of v3, /device:TPU:1, one launch (start us, length us, event | category | flops | bytes accessed | tf_op | source)
XLA Modules:
  0.0 49.6 jit_solution(14001124945114406334)
XLA Ops:
  0.6 44.9 %resample.1 = (f32[1,128]{1,0:T(1,128)}, f32[128,128]{1,0:T(8,128)}, f32[128,128]{1,0:T(8,128)}) custom-call(s32[128,128]{1,0:T(8,128)} %bitcast.4, f32[128,128]{1,0:T(8,128)} %bitcast.5, bf16[128,16384]{1,0:T(8,128)(2,1)} %args_2_.4), custom_call_target="tpu_custom_call" | custom-call | tf_op jit(solution)/shard_map/resample/pallas_call | solution.py:483
  45.5 1.2 %copy.9 = f32[128]{0:T(128)} copy(f32[128]{0:T(128)} %bitcast.7) | data formatting | bytes 1024
  46.7 1.5 %copy.10 = f32[128,128]{1,0:T(8,128)} copy(f32[128,128]{1,0:T(8,128)} %get-tuple-element.13) | data formatting | bytes 131072
  48.1 1.5 %copy.11 = f32[16384]{0:T(1024)} copy(f32[16384]{0:T(1024)} %bitcast.6) | data formatting | bytes 131072

commit v4 on v3

--- a/solution.py
+++ b/solution.py
@@ -10,8 +10,10 @@
 FLOOR = -10000.0
 COUNT = 16384
 STATE = 128
-GRAIN = 32
-PHASES = (64, 32, 32)
+GRAIN = 64
+PHASES = (2, 2, 2, 1, 1)
+JOIN_AT = (24, 24, 24, 40)
+UNROLL = 8
 CHIPS = 16
 GROUP = 32
 CHUNKS = COUNT // 256
@@ -202,7 +204,6 @@
                             device_id_type=pl.DeviceIdType.MESH)
     loads[0].wait()
     loads[1].wait()
-
     tops = own_tops(bins_ref, weights_ref, refs["marks"])
     for r in range(16):
         rows = pl.ds(8 * r, 8)
@@ -224,9 +225,12 @@
     iota_ref = refs["iota"]
     iota_ref[...] = lax.broadcasted_iota(jnp.int32, (256, 128), 0).astype(jnp.float32).astype(jnp.bfloat16)
     loads[2].wait()
-    pl.semaphore_wait(barrier, GROUP - 1)
-
-    def push(chunk, register):
+
+    def push(chunk, register, stored):
+        if stored:
+            for q in range(2):
+                pltpu.matmul_push_rhs(refs["hot"][q, chunk], staging_register=register, mxu_index=q)
+            return
         scaled = tile_of(rows_of(refs["scaled"], chunk))
         for q in range(2):
             key = tile_of(rows_of(refs["key%d" % q], chunk))
@@ -235,14 +239,22 @@
                 lanes = slice(128 * side, 128 * side + 128)
                 key_full = jnp.concatenate([key[:, lanes]] * 16, axis=0)
                 scaled_full = jnp.concatenate([scaled[:, lanes]] * 16, axis=0)
-                halves.append(jnp.where(iota_ref[...] == key_full, scaled_full, jnp.bfloat16(0)))
+                half = jnp.where(iota_ref[...] == key_full, scaled_full, jnp.bfloat16(0))
+                refs["hot"][q, chunk, lanes, :] = half.T
+                halves.append(half)
             pltpu.matmul_push_rhs(jnp.concatenate(halves, axis=1), staging_register=register,
                                   mxu_index=q, transpose=True)
 
     near_copies, tab_copy = [], []
 
+    def parts_of(h):
+        if h < 3:
+            row = ((chip >> 2) + (2, 1, 3)[h]) & 3
+            return [2 * row, 2 * row + 1]
+        return [(chip >> 1) ^ 1] if h == 3 else [chip >> 1]
+
     def send_near(h):
-        c = copy(refs["sums%d" % h].at[:, 1 - core], refs["near%d" % h], refs["near_send"].at[h],
+        c = copy(refs["sums%d" % h].at[:, :, 1 - core], refs["near%d" % h], refs["near_send"].at[h],
                  refs["near_recv"].at[h], mate)
         c.start()
         near_copies.append(c)
@@ -254,21 +266,30 @@
 
     sum_copies, note_copies, word_copies = [], [], []
 
+    def send_sums(h, u, q, where):
+        slot = 4 * h + (chip & 3) if h < 3 else (12 + (chip & 1) if h == 3 else 14)
+        c = copy(refs["merged%d" % h].at[u, q], refs["got"].at[slot], refs["sum_send"].at[slot_of(h, u, q)],
+                 refs["sum_recv"].at[slot], 2 * where + core)
+        c.start()
+        sum_copies.append(c)
+
+    def slot_of(h, u, q):
+        return 4 * h + 2 * u + q if h < 3 else (12 + q if h == 3 else 14)
+
     def join(h):
         near_copies[h].wait()
         sums, near, merged = refs["sums%d" % h], refs["near%d" % h], refs["merged%d" % h]
-        for c in range(CHIPS):
-            merged[c] = (sums[c, core] * refs["fac"][c:c + 1, :] + near[c] * refs["mate"][c:c + 1, :])
-
-    def send_sums(h):
-        sent = []
-        for j, off in enumerate(ORDER):
-            where = chip_at(off)
-            c = copy(refs["merged%d" % h].at[where], refs["got%d" % h].at[j], refs["sum_send%d" % h].at[j],
-                     refs["sum_recv%d" % h].at[j], 2 * where + core)
-            c.start()
-            sent.append(c)
-        sum_copies.append(sent)
+        ready = []
+        for u, p in enumerate(parts_of(h)):
+            for q in ((0, 1) if h < 4 else (1 - (chip & 1), chip & 1)):
+                where = 2 * p + q
+                row = pl.ds(where, 1)
+                merged[u, q] = (sums[u, q, core] * refs["fac"][row, :]
+                                + near[u, q] * refs["mate"][row, :])
+                ready.append((u, q, where))
+                if h < 4 and len(ready) > 1:
+                    send_sums(h, *ready[-2])
+        send_sums(h, *(ready[-1] if h < 4 else ready[0]))
 
     def join_tops():
         tab_copy[0].wait()
@@ -285,15 +306,20 @@
     def send_notes():
         for j, off in enumerate(ORDER):
             where = chip_at(off)
-            c = copy(note_ref.at[where], got_note.at[j], refs["note_send"].at[j], refs["note_recv"].at[j],
-                     2 * where + core)
+            c = copy(note_ref.at[where], got_note.at[chip], refs["note_send"].at[j],
+                     refs["note_recv"].at[chip], 2 * where + core)
             c.start()
             note_copies.append(c)
-        got_note[CHIPS - 1] = note_ref[chip]
+        got_note[chip] = note_ref[chip]
+
+    def arrived(dst, recv):
+        copy(dst, dst, refs["note_send"].at[0], recv, mate).wait_recv()
 
     def join_notes():
         for c in note_copies:
-            c.wait()
+            c.wait_send()
+        for off in ORDER:
+            arrived(got_note.at[chip_at(off)], refs["note_recv"].at[chip_at(off)])
         tops = got_note[:, 0, :]
         bin_top = jnp.max(tops, axis=0, keepdims=True)
         factor = jnp.exp(tops - bin_top)
@@ -330,35 +356,43 @@
         cum_ref[...] = (before + run) / total
         out_ref[...] = jnp.exp(weights_ref[...] - top_all) * (whole / total)
 
-    def gather_sums(h, start):
-        acc = refs["merged%d" % h][chip] * refs["factor"][CHIPS - 1:CHIPS, :]
-        for j, c in enumerate(sum_copies[h]):
-            c.wait()
-            acc = acc + refs["got%d" % h][j] * refs["factor"][j:j + 1, :]
-        means_ref[start:start + PHASES[h], :] = acc / jnp.maximum(refs["owned"][1:2, :], 1.0)
-
-    most = max(PHASES) // GRAIN
+    def gather_sums():
+        acc = refs["merged4"][0, chip & 1] * refs["factor"][pl.ds(chip, 1), :]
+        for slot in range(15):
+            if slot < 12:
+                source = ((((chip >> 2) - (2, 1, 3)[slot // 4]) & 3) << 2) | (slot & 3)
+            elif slot < 14:
+                source = (chip ^ 2) & 14 | (slot & 1)
+            else:
+                source = chip ^ 1
+            arrived(refs["got"].at[slot], refs["sum_recv"].at[slot])
+            acc = acc + refs["got"][slot] * refs["factor"][pl.ds(source, 1), :]
+        for c in sum_copies:
+            c.wait_send()
+        means_ref[...] = acc / jnp.maximum(refs["owned"][1:2, :], 1.0)
+
+    grains = STATE // GRAIN
 
     def run(*accs):
-        size = 8 * most + 1
+        size = 2 * grains + 1
         accs = (accs[:size], accs[size:])
 
         def multiply(chunk, register, h):
-            part = tile_of(rows_of(refs["part"], chunk))
+            part = jnp.broadcast_to(rows_of(refs["part"], chunk), (16, 256))
             cols = pl.ds(pl.multiple_of(chunk * 256, 256), 256)
             first = register
-            for g in range(PHASES[h] // GRAIN):
-                block = states_ref[pl.ds(sum(PHASES[:h]) + g * GRAIN, GRAIN), cols]
-                for p in range(8):
-                    mask = jnp.where(part == p, jnp.bfloat16(1), jnp.bfloat16(0))
-                    lhs = block * jnp.concatenate([mask] * (GRAIN // 16), axis=0)
+            for u, p in enumerate(parts_of(h)):
+                mask = jnp.where(part == p.astype(jnp.float32), 1.0, 0.0).astype(jnp.bfloat16)
+                mask = jnp.concatenate([mask] * (GRAIN // 16), axis=0)
+                for g in range(grains):
+                    lhs = states_ref[pl.ds(g * GRAIN, GRAIN), cols] * mask
                     for q in range(2):
-                        pltpu.matmul_acc_lhs(accs[q][g * 8 + p], lhs, load_staged_rhs=first)
+                        pltpu.matmul_acc_lhs(accs[q][u * grains + g], lhs, load_staged_rhs=first)
                     first = None
             if h == 0:
                 row = lax.broadcasted_iota(jnp.int32, (16, 256), 0)
                 lower = row < 8
-                mine = (row & 7).astype(jnp.float32) == jnp.broadcast_to(rows_of(refs["part"], chunk), (16, 256))
+                mine = (row & 7).astype(jnp.float32) == part
                 flag, t1, t2, t3 = (
                     jnp.broadcast_to(rows_of(refs[name], chunk), (16, 256))
                     for name in ("flag", "t1", "t2", "t3")
@@ -370,20 +404,19 @@
                     pltpu.matmul_acc_lhs(accs[q][size - 1], lhs)
 
         def chunks(h, start, stop):
-            @pl.loop(start, stop, step=2)
+            @pl.loop(start, stop, step=UNROLL)
             def _(chunk):
-                multiply(chunk, 0, h)
-                push(chunk + 1, 1)
-                multiply(chunk + 1, 1, h)
-                push((chunk + 2) & (CHUNKS - 1), 0)
+                for k in range(UNROLL):
+                    multiply(chunk + k, k & 1, h)
+                    push((chunk + k + 1) & (CHUNKS - 1), 1 - (k & 1), h > 0)
 
         def drain(h):
-            for g in range(PHASES[h] // GRAIN):
-                for p in range(8):
+            for u in range(PHASES[h]):
+                for g in range(grains):
                     for q in range(2):
-                        got = pltpu.matmul_pop(accs[q][g * 8 + p])
+                        got = pltpu.matmul_pop(accs[q][u * grains + g])
                         for side in range(2):
-                            refs["sums%d" % h][2 * p + q, side, GRAIN * g:GRAIN * g + GRAIN, :] = (
+                            refs["sums%d" % h][u, q, side, GRAIN * g:GRAIN * g + GRAIN, :] = (
                                 got[:, 128 * side:128 * side + 128])
 
         def drain_tops():
@@ -404,46 +437,44 @@
         for q in range(2):
             for a in accs[q]:
                 pltpu.matmul_pop(a)
-        push(0, 0)
+        push(0, 0, False)
         chunks(0, 0, CHUNKS)
         drain_tops()
         drain(0)
-        send_tab()
-        send_near(0)
-        chunks(1, 0, SPLIT[0])
-        join_tops()
-        join(0)
-        send_notes()
-        send_sums(0)
-        chunks(1, SPLIT[0], CHUNKS)
-        drain(1)
-        send_near(1)
-        chunks(2, 0, SPLIT[1])
-        join(1)
-        join_notes()
-        send_sums(1)
-        send_words()
-        chunks(2, SPLIT[1], CHUNKS)
-        drain(2)
+        for h in range(1, len(PHASES)):
+            stop = JOIN_AT[h - 1]
+            chunks(h, 0, UNROLL)
+            if h == 1:
+                pl.semaphore_wait(barrier, GROUP - 1)
+                send_tab()
+            send_near(h - 1)
+            chunks(h, UNROLL, stop)
+            if h == 1:
+                join_tops()
+            if h == 3:
+                join_notes()
+            join(h - 1)
+            if h == 1:
+                send_notes()
+            if h == 3:
+                send_words()
+            chunks(h, stop, CHUNKS)
+            drain(h)
         for q in range(2):
             pltpu.matmul_acc_lhs(accs[q][size - 1], jnp.zeros((48, 256), jnp.bfloat16), load_staged_rhs=0)
             pltpu.matmul_pop(accs[q][size - 1])
-        send_near(2)
+        send_near(len(PHASES) - 1)
+        join(len(PHASES) - 1)
         join_words()
-        join(2)
-        gather_sums(0, 0)
-        send_sums(2)
-        gather_sums(1, PHASES[0])
-        gather_sums(2, PHASES[0] + PHASES[1])
+        gather_sums()
 
     specs = []
     for q in range(2):
-        specs += [pltpu.ACC(q)((GRAIN, 256), jnp.float32)] * (8 * most) + [pltpu.ACC(q)((48, 256), jnp.float32)]
+        specs += [pltpu.ACC(q)((GRAIN, 256), jnp.float32)] * (2 * grains) + [pltpu.ACC(q)((48, 256), jnp.float32)]
     pl.run_scoped(run, *specs)
 
 
-SPLIT = (32, 32)
-VMEM_LIMIT = 67043328
+VMEM_LIMIT = 55040 * 1024
 
 
 def scratch():
@@ -451,7 +482,7 @@
     table = pltpu.VMEM((128, 128), f32)
     shapes = dict(
         bins=pltpu.VMEM((128, 128), jnp.int32), weights=table,
-        states=pltpu.VMEM((STATE, COUNT), bf16), marks=pltpu.VMEM((MARKS, 8, 128), jnp.int32),
+        states=pltpu.VMEM((STATE, COUNT), bf16), hot=pltpu.VMEM((2, CHUNKS, 256, 256), bf16), marks=pltpu.VMEM((MARKS, 8, 128), jnp.int32),
         iota=pltpu.VMEM((256, 128), bf16), scaled=table, key0=table, key1=table, part=table,
         flag=table, t1=table, t2=table, t3=table,
         tab=pltpu.VMEM((2 * GROUP, 128), f32), near_tab=pltpu.VMEM((2 * GROUP, 128), f32),
@@ -463,12 +494,13 @@
         tab_send=dma, tab_recv=dma, note_send=dma((CHIPS,)), note_recv=dma((CHIPS,)),
         word_send=dma((GROUP,)), word_recv=dma((GROUP,)),
     )
-    for h, rows in enumerate(PHASES):
-        shapes["sums%d" % h] = pltpu.VMEM((CHIPS, 2, rows, 128), f32)
-        for name in ("near", "merged", "got"):
-            shapes["%s%d" % (name, h)] = pltpu.VMEM((CHIPS, rows, 128), f32)
-        shapes["sum_send%d" % h] = dma((CHIPS,))
-        shapes["sum_recv%d" % h] = dma((CHIPS,))
+    for h, count in enumerate(PHASES):
+        shapes["sums%d" % h] = pltpu.VMEM((count, 2, 2, STATE, 128), f32)
+        for name in ("near", "merged"):
+            shapes["%s%d" % (name, h)] = pltpu.VMEM((count, 2, STATE, 128), f32)
+    shapes["got"] = pltpu.VMEM((CHIPS, STATE, 128), f32)
+    shapes["sum_send"] = dma((CHIPS,))
+    shapes["sum_recv"] = dma((CHIPS,))
     return shapes
 
 

time: 50 us -> 43.5 us (0.87)
  Pallas kernels: 44.9 us -> 40.9 us
  local copies, waits for them, and re-layouts: 4.12 us -> 1.78 us
    pallas_call x1, Pallas kernels: 44.9 us -> 40.9 us  [body(): pl.pallas_call(call, out_shape=(jax.ShapeDtypeStruct((1, 128), jnp.float3...]
    unnamed x3, local copies, waits for them, and re-layouts: 4.12 us -> 1.78 us
where the time goes in v4:
time: 43.5 us; the launch traced here: 43.3 us
  Pallas kernels  40.9 us (94%)
  local copies, waits for them, and re-layouts  1.78 us (4%)
  between operations  0.64 us (1%)
    pallas_call x1, Pallas kernels, body(): pl.pallas_call(call, out_shape=(jax.ShapeDtypeStruct((1, 128), jnp.float3...  40.9 us
    unnamed x3, local copies, waits for them, and re-layouts  1.78 us

profile of v4, /device:TPU:1, one launch (start us, length us, event | category | flops | bytes accessed | tf_op | source)
XLA Modules:
  0.0 43.3 jit_solution(18443973014372275370)
XLA Ops:
  0.6 40.9 %resample.1 = (f32[1,128]{1,0:T(1,128)S(1)}, f32[128,128]{1,0:T(8,128)S(1)}, f32[128,128]{1,0:T(8,128)S(1)}) custom-call(s32[128,128]{1,0:T(8,128)} %bitcast.6, f32[128,128]{1,0:T(8,128)} %bitcast.7, bf16[128,16384]{1,0:T(8,128)(2,1)} %args_2_.4), custom_call_target="tpu_custom_call" | custom-call | tf_op jit(solution)/shard_map/resample/pallas_call | solution.py:515
  41.6 0.5 %copy.9 = f32[128]{0:T(128)} copy(f32[128]{0:T(128)S(1)} %bitcast.5) | data formatting | bytes 1024
  42.1 0.6 %copy.10 = f32[128,128]{1,0:T(8,128)} copy(f32[128,128]{1,0:T(8,128)S(1)} %get-tuple-element.13) | data formatting | bytes 131072
  42.7 0.6 %copy.11 = f32[16384]{0:T(1024)} copy(f32[16384]{0:T(1024)S(1)} %bitcast.4) | data formatting | bytes 131072

commit v5 on v4

--- a/solution.py
+++ b/solution.py
@@ -11,9 +11,9 @@
 COUNT = 16384
 STATE = 128
 GRAIN = 64
-PHASES = (2, 2, 2, 1, 1)
-JOIN_AT = (24, 24, 24, 40)
-UNROLL = 8
+WIDE = 3
+NEAR = (2, 3, 1, 0)
+PHASES = WIDE + len(NEAR)
 CHIPS = 16
 GROUP = 32
 CHUNKS = COUNT // 256
@@ -100,37 +100,36 @@
 
 
 def shifted(vecs, by):
-    step = abs(by)
-    sign = 1 if by > 0 else -1
-    if step >= 128:
-        return [rotate(x, by // 128, 1) for x in vecs]
-    sublane = lax.broadcasted_iota(jnp.int32, (8, 128), 0)
-
-    def carry_sub(x, m):
-        moved = rotate(x, m, 0)
-        crossed = rotate(moved, sign, 1)
-        inside = (sublane + m < 8) if m > 0 else (sublane + m >= 0)
-        return jnp.where(inside, moved, crossed)
-
-    if step >= 16:
-        return [carry_sub(x, by // 16) for x in vecs]
-    out = []
-    for r in range(16):
-        q = r + by
-        out.append(vecs[q] if 0 <= q < 16 else carry_sub(vecs[q % 16], sign))
-    return out
+    if abs(by) >= 16:
+        return [rotate(x, by // 16, 0) for x in vecs]
+    return [
+        vecs[r + by] if 0 <= r + by < 16 else rotate(vecs[(r + by) % 16], 1 if by > 0 else -1, 0)
+        for r in range(16)
+    ]
 
 
 def segment_tops(groups, vals):
     for sign in (1, -1):
-        for level in range(14):
+        for level in range(7):
             by = sign * (1 << level)
             near_groups, near_vals = shifted(groups, by), shifted(vals, by)
             vals = [
                 jnp.where(g == ng, jnp.maximum(v, nv), v)
                 for g, ng, v, nv in zip(groups, near_groups, vals, near_vals)
             ]
-    return vals
+    first, last = (jnp.broadcast_to(x, (8, 128)) for x in (groups[0][0:1], groups[15][7:8]))
+    first_top, last_top = (jnp.broadcast_to(x, (8, 128)) for x in (vals[0][0:1], vals[15][7:8]))
+    left, right = last_top, first_top
+    for level in range(7):
+        by = 1 << level
+        left = jnp.where(rotate(last, -by, 1) == last, jnp.maximum(left, rotate(left, -by, 1)), left)
+        right = jnp.where(rotate(first, by, 1) == first, jnp.maximum(right, rotate(right, by, 1)), right)
+    left = jnp.where(rotate(last, -1, 1) == first, rotate(left, -1, 1), FLOOR)
+    right = jnp.where(rotate(first, 1, 1) == last, rotate(right, 1, 1), FLOOR)
+    return [
+        jnp.maximum(v, jnp.maximum(jnp.where(g == first, left, FLOOR), jnp.where(g == last, right, FLOOR)))
+        for g, v in zip(groups, vals)
+    ]
 
 
 def own_tops(bins_ref, weights_ref, mark_ref):
@@ -226,11 +225,17 @@
     iota_ref[...] = lax.broadcasted_iota(jnp.int32, (256, 128), 0).astype(jnp.float32).astype(jnp.bfloat16)
     loads[2].wait()
 
-    def push(chunk, register, stored):
-        if stored:
+    def push(h, step, register):
+        if h >= WIDE:
+            q = target_of(h) & 1
+            for m in range(2):
+                pltpu.matmul_push_rhs(refs["hot"][q, 2 * step + m], staging_register=register, mxu_index=m)
+            return
+        if h:
             for q in range(2):
-                pltpu.matmul_push_rhs(refs["hot"][q, chunk], staging_register=register, mxu_index=q)
+                pltpu.matmul_push_rhs(refs["hot"][q, step], staging_register=register, mxu_index=q)
             return
+        chunk = step
         scaled = tile_of(rows_of(refs["scaled"], chunk))
         for q in range(2):
             key = tile_of(rows_of(refs["key%d" % q], chunk))
@@ -247,15 +252,21 @@
 
     near_copies, tab_copy = [], []
 
+    row, column = chip >> 2, chip & 3
+
     def parts_of(h):
-        if h < 3:
-            row = ((chip >> 2) + (2, 1, 3)[h]) & 3
-            return [2 * row, 2 * row + 1]
-        return [(chip >> 1) ^ 1] if h == 3 else [chip >> 1]
+        if h == 0:
+            away = 2 * ((row + 2) & 3)
+            return [away, away + 1]
+        return [2 * ((row + by) & 3) + ((column >> 1) ^ (h & 1)) for by in (1, 3)]
+
+    def target_of(h):
+        return chip ^ NEAR[h - WIDE]
 
     def send_near(h):
-        c = copy(refs["sums%d" % h].at[:, :, 1 - core], refs["near%d" % h], refs["near_send"].at[h],
-                 refs["near_recv"].at[h], mate)
+        sums = refs["sums%d" % h]
+        c = copy(sums.at[:, :, 1 - core] if h < WIDE else sums.at[1 - core], refs["near%d" % h],
+                 refs["near_send"].at[h], refs["near_recv"].at[h], mate)
         c.start()
         near_copies.append(c)
 
@@ -266,30 +277,34 @@
 
     sum_copies, note_copies, word_copies = [], [], []
 
-    def send_sums(h, u, q, where):
-        slot = 4 * h + (chip & 3) if h < 3 else (12 + (chip & 1) if h == 3 else 14)
-        c = copy(refs["merged%d" % h].at[u, q], refs["got"].at[slot], refs["sum_send"].at[slot_of(h, u, q)],
-                 refs["sum_recv"].at[slot], 2 * where + core)
+    def send_sums(src, send, slot, where):
+        c = copy(src, refs["got"].at[slot], refs["sum_send"].at[send], refs["sum_recv"].at[slot],
+                 2 * where + core)
         c.start()
         sum_copies.append(c)
-
-    def slot_of(h, u, q):
-        return 4 * h + 2 * u + q if h < 3 else (12 + q if h == 3 else 14)
 
     def join(h):
         near_copies[h].wait()
         sums, near, merged = refs["sums%d" % h], refs["near%d" % h], refs["merged%d" % h]
+        if h >= WIDE:
+            where = target_of(h)
+            at = pl.ds(where, 1)
+            merged[...] = sums[core] * refs["fac"][at, :] + near[...] * refs["mate"][at, :]
+            if h < PHASES - 1:
+                send_sums(merged, 4 * WIDE + h - WIDE, 4 * WIDE + h - WIDE, where)
+            return
         ready = []
         for u, p in enumerate(parts_of(h)):
-            for q in ((0, 1) if h < 4 else (1 - (chip & 1), chip & 1)):
+            for q in range(2):
                 where = 2 * p + q
-                row = pl.ds(where, 1)
-                merged[u, q] = (sums[u, q, core] * refs["fac"][row, :]
-                                + near[u, q] * refs["mate"][row, :])
-                ready.append((u, q, where))
-                if h < 4 and len(ready) > 1:
-                    send_sums(h, *ready[-2])
-        send_sums(h, *(ready[-1] if h < 4 else ready[0]))
+                at = pl.ds(where, 1)
+                merged[u, q] = (sums[u, q, core] * refs["fac"][at, :]
+                                + near[u, q] * refs["mate"][at, :])
+                slot = column if h == 0 else 4 * h + 2 * u + (column & 1)
+                ready.append((merged.at[u, q], 4 * h + 2 * u + q, slot, where))
+                if len(ready) > 1:
+                    send_sums(*ready[-2])
+        send_sums(*ready[-1])
 
     def join_tops():
         tab_copy[0].wait()
@@ -327,9 +342,8 @@
         refs["factor"][...] = factor
         refs["owned"][0:1, :] = bin_top
         refs["owned"][1:2, :] = bin_mass
-        block_top = lane_max(bin_top)
-        word_ref[0:1, :] = block_top
-        word_ref[1:2, :] = lane_sum(bin_mass * jnp.exp(bin_top - block_top))
+        word_ref[0:1, :] = bin_top
+        word_ref[1:2, :] = bin_mass
         words_ref[0] = word_ref[...]
 
     def send_words():
@@ -343,11 +357,11 @@
         for c in word_copies:
             c.wait()
         all_tops, all_masses = words_ref[:, 0, :], words_ref[:, 1, :]
-        top_all = jnp.max(all_tops, axis=0, keepdims=True)
+        top_all = lane_max(jnp.max(all_tops, axis=0, keepdims=True))
         scaled = all_masses * jnp.exp(all_tops - top_all)
-        total = jnp.sum(scaled, axis=0, keepdims=True)
+        total = lane_sum(jnp.sum(scaled, axis=0, keepdims=True))
         at = lax.broadcasted_iota(jnp.int32, (GROUP, 128), 0)
-        before = jnp.sum(jnp.where((at >= 1) & (at <= me), scaled, 0.0), axis=0, keepdims=True)
+        before = lane_sum(jnp.sum(jnp.where((at >= 1) & (at <= me), scaled, 0.0), axis=0, keepdims=True))
         run = refs["owned"][1:2, :] * jnp.exp(refs["owned"][0:1, :] - top_all)
         lane = lax.broadcasted_iota(jnp.int32, (1, 128), 1)
         for level in range(7):
@@ -357,14 +371,15 @@
         out_ref[...] = jnp.exp(weights_ref[...] - top_all) * (whole / total)
 
     def gather_sums():
-        acc = refs["merged4"][0, chip & 1] * refs["factor"][pl.ds(chip, 1), :]
-        for slot in range(15):
-            if slot < 12:
-                source = ((((chip >> 2) - (2, 1, 3)[slot // 4]) & 3) << 2) | (slot & 3)
-            elif slot < 14:
-                source = (chip ^ 2) & 14 | (slot & 1)
+        acc = refs["merged%d" % (PHASES - 1)][...] * refs["factor"][pl.ds(chip, 1), :]
+        for slot in range(CHIPS - 1):
+            if slot < 4:
+                source = (((row - 2) & 3) << 2) | slot
+            elif slot < 4 * WIDE:
+                source = (((row - (1, 3)[slot // 2 % 2]) & 3) << 2) | (
+                    (column ^ (2 if slot < 8 else 0)) & 2) | (slot & 1)
             else:
-                source = chip ^ 1
+                source = chip ^ NEAR[slot - 4 * WIDE]
             arrived(refs["got"].at[slot], refs["sum_recv"].at[slot])
             acc = acc + refs["got"][slot] * refs["factor"][pl.ds(source, 1), :]
         for c in sum_copies:
@@ -374,25 +389,37 @@
     grains = STATE // GRAIN
 
     def run(*accs):
-        size = 2 * grains + 1
+        size = 6 * grains + 1
         accs = (accs[:size], accs[size:])
 
-        def multiply(chunk, register, h):
+        def factors(chunk, p):
             part = jnp.broadcast_to(rows_of(refs["part"], chunk), (16, 256))
+            mask = jnp.where(part == p.astype(jnp.float32), 1.0, 0.0).astype(jnp.bfloat16)
+            mask = jnp.concatenate([mask] * (GRAIN // 16), axis=0)
             cols = pl.ds(pl.multiple_of(chunk * 256, 256), 256)
+            return [states_ref[pl.ds(g * GRAIN, GRAIN), cols] * mask for g in range(grains)]
+
+        def acc_of(h, q, u, g):
+            return accs[q][(2 * (h & 1) + u if h < WIDE else 4 + (h & 1)) * grains + g]
+
+        def multiply(h, chunk, register):
+            if h >= WIDE:
+                for m in range(2):
+                    for g, lhs in enumerate(factors(2 * chunk + m, target_of(h) >> 1)):
+                        pltpu.matmul_acc_lhs(acc_of(h, m, 0, g), lhs,
+                                             load_staged_rhs=register if g == 0 else None)
+                return
+            part = jnp.broadcast_to(rows_of(refs["part"], chunk), (16, 256))
             first = register
             for u, p in enumerate(parts_of(h)):
-                mask = jnp.where(part == p.astype(jnp.float32), 1.0, 0.0).astype(jnp.bfloat16)
-                mask = jnp.concatenate([mask] * (GRAIN // 16), axis=0)
-                for g in range(grains):
-                    lhs = states_ref[pl.ds(g * GRAIN, GRAIN), cols] * mask
+                for g, lhs in enumerate(factors(chunk, p)):
                     for q in range(2):
-                        pltpu.matmul_acc_lhs(accs[q][u * grains + g], lhs, load_staged_rhs=first)
+                        pltpu.matmul_acc_lhs(acc_of(h, q, u, g), lhs, load_staged_rhs=first)
                     first = None
             if h == 0:
-                row = lax.broadcasted_iota(jnp.int32, (16, 256), 0)
-                lower = row < 8
-                mine = (row & 7).astype(jnp.float32) == part
+                at = lax.broadcasted_iota(jnp.int32, (16, 256), 0)
+                lower = at < 8
+                mine = (at & 7).astype(jnp.float32) == part
                 flag, t1, t2, t3 = (
                     jnp.broadcast_to(rows_of(refs[name], chunk), (16, 256))
                     for name in ("flag", "t1", "t2", "t3")
@@ -403,21 +430,55 @@
                 for q in range(2):
                     pltpu.matmul_acc_lhs(accs[q][size - 1], lhs)
 
-        def chunks(h, start, stop):
-            @pl.loop(start, stop, step=UNROLL)
-            def _(chunk):
-                for k in range(UNROLL):
-                    multiply(chunk + k, k & 1, h)
-                    push((chunk + k + 1) & (CHUNKS - 1), 1 - (k & 1), h > 0)
+        def trip(h, step, many, last=False):
+            for k in range(many):
+                multiply(h, step + k, k & 1)
+                if not last or k < many - 1:
+                    push(h, step + k + 1, 1 - (k & 1))
+                elif h < PHASES - 1:
+                    push(h + 1, 0, 0)
+
+        def phase(h, actions):
+            end = CHUNKS if h < WIDE else CHUNKS // 2
+
+            def steps(start, stop):
+                many = 8 if (stop - start) % 16 else 16
+                if stop - start == many:
+                    trip(h, start, many)
+                elif stop > start:
+                    @pl.loop(start, stop, step=many)
+                    def _(step):
+                        trip(h, step, many)
+
+            trip(h, 0, 8)
+            if h:
+                drain(h - 1)
+            at = 8
+            for step in sorted(actions):
+                steps(at, step)
+                for act in actions[step]:
+                    act()
+                at = step
+            last = 16 if (end - at) % 16 == 0 else 8
+            steps(at, end - last)
+            trip(h, end - last, last, last=True)
 
         def drain(h):
-            for u in range(PHASES[h]):
+            sums = refs["sums%d" % h]
+            for u in range(2 if h < WIDE else 1):
                 for g in range(grains):
+                    rows = slice(GRAIN * g, GRAIN * g + GRAIN)
+                    if h >= WIDE:
+                        got = pltpu.matmul_pop(acc_of(h, 0, 0, g)) + pltpu.matmul_pop(acc_of(h, 1, 0, g))
+                        for side in range(2):
+                            sums[side, rows, :] = got[:, 128 * side:128 * side + 128]
+                        continue
                     for q in range(2):
-                        got = pltpu.matmul_pop(accs[q][u * grains + g])
+                        got = pltpu.matmul_pop(acc_of(h, q, u, g))
                         for side in range(2):
-                            refs["sums%d" % h][u, q, side, GRAIN * g:GRAIN * g + GRAIN, :] = (
-                                got[:, 128 * side:128 * side + 128])
+                            sums[u, q, side, rows, :] = got[:, 128 * side:128 * side + 128]
+            if h == 0:
+                drain_tops()
 
         def drain_tops():
             for q in range(2):
@@ -437,40 +498,35 @@
         for q in range(2):
             for a in accs[q]:
                 pltpu.matmul_pop(a)
-        push(0, 0, False)
-        chunks(0, 0, CHUNKS)
-        drain_tops()
-        drain(0)
-        for h in range(1, len(PHASES)):
-            stop = JOIN_AT[h - 1]
-            chunks(h, 0, UNROLL)
-            if h == 1:
-                pl.semaphore_wait(barrier, GROUP - 1)
-                send_tab()
-            send_near(h - 1)
-            chunks(h, UNROLL, stop)
-            if h == 1:
-                join_tops()
-            if h == 3:
-                join_notes()
-            join(h - 1)
-            if h == 1:
-                send_notes()
-            if h == 3:
-                send_words()
-            chunks(h, stop, CHUNKS)
-            drain(h)
-        for q in range(2):
-            pltpu.matmul_acc_lhs(accs[q][size - 1], jnp.zeros((48, 256), jnp.bfloat16), load_staged_rhs=0)
-            pltpu.matmul_pop(accs[q][size - 1])
-        send_near(len(PHASES) - 1)
-        join(len(PHASES) - 1)
+        push(0, 0, 0)
+        phase(0, {})
+
+        def greet():
+            pl.semaphore_wait(barrier, GROUP - 1)
+            send_tab()
+
+        def near(h):
+            return functools.partial(send_near, h)
+
+        def meet(h):
+            return functools.partial(join, h)
+
+        phase(1, {8: [greet, near(0)], 24: [join_tops, send_notes, meet(0)]})
+        phase(2, {8: [near(1)], 24: [meet(1)]})
+        phase(3, {8: [near(2)], 16: [join_notes]})
+        phase(4, {8: [near(3), send_words], 16: [meet(2)]})
+        for h in range(5, PHASES):
+            phase(h, {8: [near(h - 1), meet(h - 2)]})
+        drain(PHASES - 1)
+        join(PHASES - 2)
+        send_near(PHASES - 1)
         join_words()
+        join(PHASES - 1)
         gather_sums()
 
     specs = []
     for q in range(2):
-        specs += [pltpu.ACC(q)((GRAIN, 256), jnp.float32)] * (2 * grains) + [pltpu.ACC(q)((48, 256), jnp.float32)]
+        specs += [pltpu.ACC(q)((GRAIN, 256), jnp.float32)] * (6 * grains) + [pltpu.ACC(q)((48, 256), jnp.float32)]
     pl.run_scoped(run, *specs)
 
 
@@ -490,18 +546,27 @@
         factor=pltpu.VMEM((CHIPS, 128), f32), owned=pltpu.VMEM((2, 128), f32),
         note=pltpu.VMEM((CHIPS, 2, 128), f32), got_note=pltpu.VMEM((CHIPS, 2, 128), f32),
         word=pltpu.VMEM((2, 128), f32), words=pltpu.VMEM((GROUP, 2, 128), f32),
-        load_sem=dma((3,)), near_send=dma((len(PHASES),)), near_recv=dma((len(PHASES),)),
+        load_sem=dma((3,)), near_send=dma((PHASES,)), near_recv=dma((PHASES,)),
         tab_send=dma, tab_recv=dma, note_send=dma((CHIPS,)), note_recv=dma((CHIPS,)),
         word_send=dma((GROUP,)), word_recv=dma((GROUP,)),
     )
-    for h, count in enumerate(PHASES):
-        shapes["sums%d" % h] = pltpu.VMEM((count, 2, 2, STATE, 128), f32)
+    for h in range(PHASES):
+        wide = (2, 2) if h < WIDE else ()
+        shapes["sums%d" % h] = pltpu.VMEM(wide + (2, STATE, 128), f32)
         for name in ("near", "merged"):
-            shapes["%s%d" % (name, h)] = pltpu.VMEM((count, 2, STATE, 128), f32)
+            shapes["%s%d" % (name, h)] = pltpu.VMEM(wide + (STATE, 128), f32)
     shapes["got"] = pltpu.VMEM((CHIPS, STATE, 128), f32)
     shapes["sum_send"] = dma((CHIPS,))
     shapes["sum_recv"] = dma((CHIPS,))
     return shapes
+
+
+def store_kernel(*refs):
+    copies = [pltpu.make_async_copy(refs[i], refs[3 + i], refs[6].at[i]) for i in range(3)]
+    for c in copies:
+        c.start()
+    for c in copies:
+        c.wait()
 
 
 def body(log_weights, bins, states):
@@ -526,6 +591,16 @@
                                              vmem_limit_bytes=VMEM_LIMIT),
         name="resample",
     )(bins.reshape(128, 128), log_weights.reshape(128, 128), states)
+    results = (cumulative, bin_means, particle_weights)
+    cumulative, bin_means, particle_weights = pl.pallas_call(
+        store_kernel,
+        out_shape=[jax.ShapeDtypeStruct(r.shape, r.dtype) for r in results],
+        in_specs=[vmem] * 3,
+        out_specs=[pl.BlockSpec(memory_space=pltpu.HBM)] * 3,
+        scratch_shapes=[pltpu.SemaphoreType.DMA((3,))],
+        compiler_params=pltpu.CompilerParams(vmem_limit_bytes=VMEM_LIMIT),
+        name="store",
+    )(*results)
     return cumulative.reshape(128), bin_means, particle_weights.reshape(COUNT)
 
 

time: 43.5 us -> 41.4 us (0.952)
  local copies, waits for them, and re-layouts: 1.78 us -> 0 us
    unnamed x3 -> x0, local copies, waits for them, and re-layouts: 1.78 us -> none
    pallas_call x1, Pallas kernels: 40.9 us -> 39.9 us  [body(): pl.pallas_call(call, out_shape=(jax.ShapeDtypeStruct((1, 128), jnp.float3...]
    pallas_call x0 -> x1, Pallas kernels: none -> 0.68 us  [body(): pl.pallas_call(store_kernel, out_shape=[jax.ShapeDtypeStruct(r.shape, r.d...]
where the time goes in v5:
time: 41.4 us; the launch traced here: 41.3 us
  Pallas kernels  40.5 us (98%)
  between operations  0.8 us (2%)
    pallas_call x1, Pallas kernels, body(): pl.pallas_call(call, out_shape=(jax.ShapeDtypeStruct((1, 128), jnp.float3...  39.9 us

profile of v5, /device:TPU:1, one launch (start us, length us, event | category | flops | bytes accessed | tf_op | source)
XLA Modules:
  0.0 41.3 jit_solution(8391910422371406250)
XLA Ops:
  0.6 39.9 %resample.1 = (f32[1,128]{1,0:T(1,128)S(1)}, f32[128,128]{1,0:T(8,128)S(1)}, f32[128,128]{1,0:T(8,128)S(1)}) custom-call(s32[128,128]{1,0:T(8,128)} %bitcast.4, f32[128,128]{1,0:T(8,128)} %bitcast.5, bf16[128,16384]{1,0:T(8,128)(2,1)} %args_2_.4), custom_call_target="tpu_custom_call" | custom-call | tf_op jit(solution)/shard_map/resample/pallas_call | solution.py:580
  40.5 0.7 %store.1 = (f32[1,128]{1,0:T(1,128)}, f32[128,128]{1,0:T(8,128)}, f32[128,128]{1,0:T(8,128)}) custom-call(f32[1,128]{1,0:T(1,128)S(1)} %get-tuple-element.9.refs_0_, f32[128,128]{1,0:T(8,128)S(1)} %get-tuple-element.10.refs_1_, f32[128,128]{1,0:T(8,128)S(1)} %get-tuple-element.11.refs_2_), custom_call_target="tpu_custom_call" | custom-call | tf_op jit(solution)/shard_map/store/pallas_call | solution.py:595

commit v6 on v5

--- a/solution.py
+++ b/solution.py
@@ -12,7 +12,8 @@
 STATE = 128
 GRAIN = 64
 WIDE = 3
-NEAR = (2, 3, 1, 0)
+TURN_FROM = 11
+NEAR = (3, 2, 1, 0)
 PHASES = WIDE + len(NEAR)
 CHIPS = 16
 GROUP = 32
@@ -29,28 +30,42 @@
     return x
 
 
-def is_high(bit):
-    if bit < 7:
-        return ((lax.broadcasted_iota(jnp.int32, (8, 128), 0) >> (bit - 4)) & 1) == 1
-    return ((lax.broadcasted_iota(jnp.int32, (8, 128), 1) >> (bit - 7)) & 1) == 1
+def is_high(kind, bit):
+    return ((lax.broadcasted_iota(jnp.int32, (8, 128), kind) >> bit) & 1) == 1
 
 
 def network():
     steps = []
+    turned = False
     for k in range(1, 15):
-        steps.append((1 << k) - 1)
-        for j in range(k - 2, -1, -1):
-            steps.append(1 << j)
+        flips = [((1 << k) - 1, k - 1)] + [(1 << j, j) for j in range(k - 2, -1, -1)]
+        for flip, bit in flips:
+            turn = k >= TURN_FROM and bit >= 7
+            row, lane = flip & 127, flip >> 7
+            if turn:
+                step = (lane >> 3, lane & 7, (row & 15) << 3 | row >> 4)
+                top = (0, bit - 7) if bit < 10 else (2, bit - 10)
+            else:
+                step = (row & 15, row >> 4, lane)
+                top = (2, bit) if bit < 4 else ((0, bit - 4) if bit < 7 else (1, bit - 7))
+            steps.append((turn != turned,) + step + top)
+            turned = turn
     return steps
 
 
-def swap_step(keys, vals, flip, mark_ref, slot):
-    top_bit = flip.bit_length() - 1
-    vec, sub, lane = flip & 15, (flip >> 4) & 7, flip >> 7
+def turn_square(vecs):
+    square = jnp.concatenate(vecs, axis=0).T
+    return [square[8 * r:8 * r + 8] for r in range(16)]
+
+
+def swap_step(keys, vals, step, mark_ref, slot):
+    turn, vec, sub, lane, kind, bit = step
+    if turn:
+        keys, vals = turn_square(keys), turn_square(vals)
     keys, vals = list(keys), list(vals)
     if not sub and not lane:
         for r in range(16):
-            if (r >> top_bit) & 1:
+            if (r >> bit) & 1:
                 continue
             q = r ^ vec
             swap = keys[r] > keys[q]
@@ -59,13 +74,15 @@
             keys[r], keys[q] = jnp.where(swap, keys[q], keys[r]), jnp.where(swap, keys[r], keys[q])
             vals[r], vals[q] = jnp.where(swap, vals[q], vals[r]), jnp.where(swap, vals[r], vals[q])
         return keys, vals, slot
-    high = is_high(top_bit)
     other_keys = [shuffle(x, sub, lane) for x in keys]
     other_vals = [shuffle(x, sub, lane) for x in vals]
     out_keys, out_vals = [], []
     for r in range(16):
         q = r ^ vec
-        take = (keys[r] > other_keys[q]) ^ high
+        if kind == 2:
+            take = (keys[r] < other_keys[q]) if (r >> bit) & 1 else (keys[r] > other_keys[q])
+        else:
+            take = (keys[r] > other_keys[q]) ^ is_high(kind, bit)
         mark_ref[slot] = take.astype(jnp.int32)
         slot += 1
         out_keys.append(jnp.where(take, other_keys[q], keys[r]))
@@ -73,24 +90,24 @@
     return out_keys, out_vals, slot
 
 
-def undo_step(vals, flip, mark_ref, slot):
-    top_bit = flip.bit_length() - 1
-    vec, sub, lane = flip & 15, (flip >> 4) & 7, flip >> 7
+def undo_step(vals, step, mark_ref, slot):
+    turn, vec, sub, lane, kind, bit = step
     vals = list(vals)
     if not sub and not lane:
         slot -= 8
         at = slot
         for r in range(16):
-            if (r >> top_bit) & 1:
+            if (r >> bit) & 1:
                 continue
             q = r ^ vec
             swap = mark_ref[at] != 0
             at += 1
             vals[r], vals[q] = jnp.where(swap, vals[q], vals[r]), jnp.where(swap, vals[r], vals[q])
-        return vals, slot
-    slot -= 16
-    others = [shuffle(x, sub, lane) for x in vals]
-    return [jnp.where(mark_ref[slot + r] != 0, others[r ^ vec], vals[r]) for r in range(16)], slot
+    else:
+        slot -= 16
+        others = [shuffle(x, sub, lane) for x in vals]
+        vals = [jnp.where(mark_ref[slot + r] != 0, others[r ^ vec], vals[r]) for r in range(16)]
+    return (turn_square(vals) if turn else vals), slot
 
 
 def rotate(x, by, axis):
@@ -141,16 +158,16 @@
         keys.append(bins_ref[rows, :] * COUNT + (lane * 128 + sublane * 16 + r))
         vals.append(weights_ref[rows, :])
     slot = 0
-    for flip in network():
-        keys, vals, slot = swap_step(keys, vals, flip, mark_ref, slot)
+    for step in network():
+        keys, vals, slot = swap_step(keys, vals, step, mark_ref, slot)
     groups = [k >> 14 for k in keys]
     vals = segment_tops(groups, vals)
-    for flip in reversed(network()):
-        vals, slot = undo_step(vals, flip, mark_ref, slot)
+    for step in reversed(network()):
+        vals, slot = undo_step(vals, step, mark_ref, slot)
     return vals
 
 
-MARKS = sum(8 if flip < 16 else 16 for flip in network())
+MARKS = sum(16 if step[2] or step[3] else 8 for step in network())
 
 
 def rows_of(ref, chunk):
@@ -513,8 +530,8 @@
 
         phase(1, {8: [greet, near(0)], 24: [join_tops, send_notes, meet(0)]})
         phase(2, {8: [near(1)], 24: [meet(1)]})
-        phase(3, {8: [near(2)], 16: [join_notes]})
-        phase(4, {8: [near(3), send_words], 16: [meet(2)]})
+        phase(3, {8: [near(2), join_notes], 16: [send_words]})
+        phase(4, {8: [near(3), meet(2)]})
         for h in range(5, PHASES):
             phase(h, {8: [near(h - 1), meet(h - 2)]})
         drain(PHASES - 1)

time: 41.4 us -> 40.3 us (0.973)
  Pallas kernels: 40.5 us -> 39.4 us
    pallas_call x1, Pallas kernels: 39.9 us -> 38.7 us  [body(): pl.pallas_call(call, out_shape=(jax.ShapeDtypeStruct((1, 128), jnp.float3...]
where the time goes in v6:
time: 40.3 us; the launch traced here: 40.2 us
  Pallas kernels  39.4 us (98%)
  between operations  0.8 us (2%)
    pallas_call x1, Pallas kernels, body(): pl.pallas_call(call, out_shape=(jax.ShapeDtypeStruct((1, 128), jnp.float3...  38.7 us

profile of v6, /device:TPU:1, one launch (start us, length us, event | category | flops | bytes accessed | tf_op | source)
XLA Modules:
  0.0 40.2 jit_solution(15195184142008600457)
XLA Ops:
  0.6 38.7 %resample.1 = (f32[1,128]{1,0:T(1,128)S(1)}, f32[128,128]{1,0:T(8,128)S(1)}, f32[128,128]{1,0:T(8,128)S(1)}) custom-call(s32[128,128]{1,0:T(8,128)} %bitcast.4, f32[128,128]{1,0:T(8,128)} %bitcast.5, bf16[128,16384]{1,0:T(8,128)(2,1)} %args_2_.4), custom_call_target="tpu_custom_call" | custom-call | tf_op jit(solution)/shard_map/resample/pallas_call | solution.py:597
  39.4 0.7 %store.1 = (f32[1,128]{1,0:T(1,128)}, f32[128,128]{1,0:T(8,128)}, f32[128,128]{1,0:T(8,128)}) custom-call(f32[1,128]{1,0:T(1,128)S(1)} %get-tuple-element.9.refs_0_, f32[128,128]{1,0:T(8,128)S(1)} %get-tuple-element.10.refs_1_, f32[128,128]{1,0:T(8,128)S(1)} %get-tuple-element.11.refs_2_), custom_call_target="tpu_custom_call" | custom-call | tf_op jit(solution)/shard_map/store/pallas_call | solution.py:612
